TPU v7x, 256 devices: a whole 4x4x8 slice. The times are simulated.
256 devices in a mesh: dp: 8 (over y, core), expert: 32 (over z, x).
Axes of the slice: x: 4, y: 4, z: 8, core: 2. Of those that a mesh axis runs over, the one named last changes fastest.
Arguments:
- tokens: bfloat16 [32768, 1024], P(('dp', 'expert')), may hold values from -6 to 6
- cotangent: bfloat16 [32768, 1024], P(('dp', 'expert')), may hold values from -2 to 2
- expert_ids: int32 [32768, 10], P(('dp', 'expert')), may hold values from 0 to 255, all different within a row; in each aligned block of 128 rows (0 to 127, 128 to 255, ...) at most 6 rows name the same one
- gate_weights: bfloat16 [32768, 10], P(('dp', 'expert')), may hold values from 0.019897461 to 0.29882812
- expert_weights: bfloat16 [256, 3, 1024, 512], P(('dp', 'expert')), may hold values from -0.1875 to 0.1875
- shared_weights: bfloat16 [3, 1024, 512], replicated, may hold values from -0.1875 to 0.1875
Outputs:
- grad_tokens: bfloat16 [32768, 1024], P(('dp', 'expert'))
- grad_gates: bfloat16 [32768, 10], P(('dp', 'expert'))
- grad_experts: bfloat16 [256, 3, 1024, 512], P(('dp', 'expert'))
- grad_shared: float32 [3, 1024, 512], P(None, 'dp')
Inputs may be any that keep to these rules, and one draw needn't show every extreme that they name: `expert_ids`: each token names 10 different experts. Among the 128 tokens of one device no expert is named more than 6 times, and in some device's tokens some expert is named exactly 6 times.
All inputs are finite; a program needn't handle non-finite values.
Results may differ from a plain program's by a relative error of at most 0.0052.
Values may be sent and summed in bfloat16 or wider, within the bound.
A program may use at most 128 MiB of HBM per device.

v0:
```python
import jax
import jax.numpy as jnp
from jax import lax
from jax.sharding import PartitionSpec as P


def silu_parts(pre):
    sigma = jax.nn.sigmoid(pre)
    return (pre * sigma, sigma * (1.0 + pre * (1.0 - sigma)))


def contract_rows(left, right):
    return lax.dot_general(
        left, right, (((0,), (0,)), ((), ())), preferred_element_type=jnp.float32
    )


def expert_grads(inputs, upstream, scales, weight):
    hidden_units = weight.shape[2]
    paired = jnp.concatenate([weight[0], weight[1]], axis=1)
    gate_up = jnp.dot(inputs, paired, preferred_element_type=jnp.float32)
    pre_gate = gate_up[:, :hidden_units]
    pre_up = gate_up[:, hidden_units:]
    back = jnp.dot(upstream, weight[2], preferred_element_type=jnp.float32)
    activated, slope = silu_parts(pre_gate)
    hidden = activated * pre_up
    gate_grad = jnp.sum(hidden * back, axis=1)
    scaled = scales[:, None] * back
    grad_gate_in = (scaled * pre_up * slope).astype(jnp.bfloat16)
    grad_up_in = (scaled * activated).astype(jnp.bfloat16)
    both = jnp.concatenate([grad_gate_in, grad_up_in], axis=1)
    input_grad = lax.dot_general(
        both, paired, (((1,), (1,)), ((), ())), preferred_element_type=jnp.float32
    )
    hidden_b = hidden.astype(jnp.bfloat16)
    scaled_up = (scales[:, None] * upstream.astype(jnp.float32)).astype(jnp.bfloat16)
    return (input_grad, gate_grad, grad_gate_in, grad_up_in, hidden_b, scaled_up)


def weight_terms(inputs, grad_gate_in, grad_up_in, scaled_up, hidden_b):
    return jnp.stack(
        [
            contract_rows(inputs, grad_gate_in),
            contract_rows(inputs, grad_up_in),
            contract_rows(scaled_up, hidden_b),
        ],
        axis=0,
    )


def shards(tokens, cotangent, expert_ids, gate_weights, expert_weights, shared_weights):
    tok_rows, model_width = tokens.shape
    top_count = expert_ids.shape[1]
    data_count = lax.axis_size("dp")
    expert_count = lax.axis_size("expert")
    devices = data_count * expert_count
    capacity = max(2, (6 * tok_rows * top_count + 5 * devices - 1) // (5 * devices))
    slot_total = devices * capacity
    pair_count = tok_rows * top_count
    row_ids = jnp.arange(tok_rows, dtype=jnp.int32)
    earlier_mask = (row_ids[:, None] > row_ids[None, :]).astype(jnp.bfloat16)
    padded_tokens = jnp.concatenate([tokens, jnp.zeros((1, model_width), jnp.bfloat16)], axis=0)
    padded_cotangent = jnp.concatenate(
        [cotangent, jnp.zeros((1, model_width), jnp.bfloat16)], axis=0
    )
    matches = expert_ids[:, :, None] == jnp.arange(devices, dtype=jnp.int32)
    per_token = jnp.sum(matches, axis=1).astype(jnp.bfloat16)
    before = jnp.dot(earlier_mask, per_token, preferred_element_type=jnp.float32)
    slot_index = jnp.sum(jnp.where(matches, before[:, None, :], 0.0), axis=2).astype(jnp.int32)
    position = expert_ids * capacity + slot_index
    slot_table = (
        jnp.full((slot_total,), pair_count, jnp.int32)
        .at[position.reshape(-1)]
        .set(jnp.arange(pair_count, dtype=jnp.int32))
    )
    token_index = slot_table // top_count
    padded_gates = jnp.concatenate(
        [gate_weights.reshape(-1), jnp.zeros((1,), jnp.bfloat16)], axis=0
    )
    send_tokens = padded_tokens[token_index].reshape(
        data_count, expert_count, capacity, model_width
    )
    send_cotangent = padded_cotangent[token_index].reshape(
        data_count, expert_count, capacity, model_width
    )
    send_gates = padded_gates[slot_table].reshape(data_count, expert_count, capacity)
    arrived = (
        lax.all_to_all(
            lax.all_to_all(send_tokens, "dp", split_axis=0, concat_axis=0, tiled=True),
            "expert",
            split_axis=1,
            concat_axis=1,
            tiled=True,
        ),
        lax.all_to_all(
            lax.all_to_all(send_cotangent, "dp", split_axis=0, concat_axis=0, tiled=True),
            "expert",
            split_axis=1,
            concat_axis=1,
            tiled=True,
        ),
        lax.all_to_all(
            lax.all_to_all(send_gates, "dp", split_axis=0, concat_axis=0, tiled=True),
            "expert",
            split_axis=1,
            concat_axis=1,
            tiled=True,
        ),
    )
    arrived_tokens = arrived[0].reshape(slot_total, model_width)
    routed = expert_grads(
        arrived_tokens,
        arrived[1].reshape(slot_total, model_width),
        arrived[2].reshape(slot_total).astype(jnp.float32),
        expert_weights[0],
    )
    grad_experts = weight_terms(arrived_tokens, routed[2], routed[3], routed[5], routed[4]).astype(
        jnp.bfloat16
    )[None]
    outgoing_input = (
        routed[0].astype(jnp.bfloat16).reshape(data_count, expert_count, capacity, model_width)
    )
    outgoing_gate = routed[1].astype(jnp.bfloat16).reshape(data_count, expert_count, capacity)
    returned = (
        lax.all_to_all(
            lax.all_to_all(outgoing_input, "dp", split_axis=0, concat_axis=0, tiled=True),
            "expert",
            split_axis=1,
            concat_axis=1,
            tiled=True,
        ),
        lax.all_to_all(
            lax.all_to_all(outgoing_gate, "dp", split_axis=0, concat_axis=0, tiled=True),
            "expert",
            split_axis=1,
            concat_axis=1,
            tiled=True,
        ),
    )
    flat_back = returned[0].reshape(slot_total, model_width)
    routed_sum = jnp.sum(flat_back[position].astype(jnp.float32), axis=1)
    grad_gates = returned[1].reshape(slot_total)[position]
    shared = expert_grads(tokens, cotangent, jnp.ones((tok_rows,), jnp.float32), shared_weights)
    grad_tokens = (routed_sum + shared[0]).astype(jnp.bfloat16)
    kept_rows = model_width // data_count
    local_terms = weight_terms(tokens, shared[2], shared[3], shared[5], shared[4])
    summed = lax.psum(local_terms, ("dp", "expert"))
    grad_shared = lax.dynamic_slice_in_dim(summed, lax.axis_index("dp") * kept_rows, kept_rows, 1)
    return (grad_tokens, grad_gates, grad_experts, grad_shared)


def solution(mesh):
    placed = (
        P(("dp", "expert"), None),
        P(("dp", "expert"), None),
        P(("dp", "expert"), None),
        P(("dp", "expert"), None),
        P(("dp", "expert"), None, None, None),
        P(),
    )
    return jax.shard_map(
        shards,
        mesh=mesh,
        in_specs=placed,
        out_specs=(
            P(("dp", "expert"), None),
            P(("dp", "expert"), None),
            P(("dp", "expert"), None, None, None),
            P(None, "dp", None),
        ),
        check_vma=False,
    )
```

profile of v0, /device:TPU:2, one launch (start us, length us, event | category | flops | bytes accessed | tf_op | source)
XLA Modules:
  0.0 783.6 jit_solution(2855569796462493825)
XLA Ops:
  10.5 5.2 scatter_custom_fusion
  16.8 9.5 %gather_fusion = bf16[1536]{0:T(1024)(128)(2,1)S(1)} fusion(bf16[1281]{0:T(1024)(128)(2,1)S(1)} %pad_maximum_fusion.14, s32[2048]{0:T(1024)S(1)} %get-tuple-element.38), kind=kCustom, calls=%fused_computation | custom fusion | bytes 12288 | tf_op jit(solution)/shard_map/gather | solution.py:86
  26.5 9.6 %all_to_all.50 = bf16[8,32,6]{1,2,0:T(8,128)(2,1)S(1)} all-to-all(bf16[8,32,6]{1,2,0:T(8,128)(2,1)S(1)} %copy.65), channel_id=1, replica_groups=mesh['dp'=8,'expert'=32] {'dp'}, dimensions={0} | all-to-all | bytes 6144 | tf_op jit(solution)/shard_map/all_to_all | solution.py:103
  36.9 11.6 %all-to-all-start.1 = ((bf16[8,32,6]{2,0,1:T(8,128)(2,1)}), bf16[8,32,6]{2,0,1:T(8,128)(2,1)S(1)}, u32[]{:S(2)}, u32[]{:S(2)}) async-start(bf16[8,32,6]{2,0,1:T(8,128)(2,1)} %copy.66), calls=%async_computation.1 | async-start | bytes 131072 | tf_op jit(solution)/shard_map/all_to_all | solution.py:102
  48.6 5.1 gather_fusion.2
  56.5 5.7 copy.72
  66.8 5.8 gather_fusion.1
  72.7 6.2 reshape.136
  78.9 5.7 copy.69
  84.6 19.6 %all-to-all-done.4 = bf16[8,32,6,1024]{3,1,2,0:T(8,128)(2,1)S(1)} async-done(((bf16[8,32,6,1024]{3,1,2,0:T(8,128)(2,1)}), bf16[8,32,6,1024]{3,1,2,0:T(8,128)(2,1)S(1)}, u32[]{:S(2)}, u32[]{:S(2)}) %all-to-all-start.4) | async-done | bytes 3145760 | tf_op jit(solution)/shard_map/all_to_all | solution.py:89
  112.0 35.0 %all-to-all-done.2 = bf16[8,32,6,1024]{3,1,2,0:T(8,128)(2,1)} async-done(((bf16[8,32,6,1024]{3,1,2,0:T(8,128)(2,1)}), bf16[8,32,6,1024]{3,1,2,0:T(8,128)(2,1)}, u32[]{:S(2)}, u32[]{:S(2)}) %all-to-all-start.2) | async-done | bytes 3145760 | tf_op jit(solution)/shard_map/all_to_all | solution.py:96
  147.1 9.8 %all-to-all-start.5 = ((bf16[8,32,6,1024]{3,0,2,1:T(8,128)(2,1)}), bf16[8,32,6,1024]{3,0,2,1:T(8,128)(2,1)S(1)}, u32[]{:S(2)}, u32[]{:S(2)}) async-start(bf16[8,32,6,1024]{3,0,2,1:T(8,128)(2,1)} %copy.73), calls=%async_computation.5 | async-start | bytes 6291456 | tf_op jit(solution)/shard_map/all_to_all | solution.py:88
  156.8 5.4 copy.70
  162.2 65.4 %all-to-all-done.5 = bf16[8,32,6,1024]{3,0,2,1:T(8,128)(2,1)S(1)} async-done(((bf16[8,32,6,1024]{3,0,2,1:T(8,128)(2,1)}), bf16[8,32,6,1024]{3,0,2,1:T(8,128)(2,1)S(1)}, u32[]{:S(2)}, u32[]{:S(2)}) %all-to-all-start.5) | async-done | bytes 3145760 | tf_op jit(solution)/shard_map/all_to_all | solution.py:88
  227.6 7.5 all-to-all-start.3
  242.4 4.9 reshape.139
  247.3 58.2 %all-to-all-done.3 = bf16[8,32,6,1024]{3,0,2,1:T(8,128)(2,1)} async-done(((bf16[8,32,6,1024]{3,0,2,1:T(8,128)(2,1)}), bf16[8,32,6,1024]{3,0,2,1:T(8,128)(2,1)}, u32[]{:S(2)}, u32[]{:S(2)}) %all-to-all-start.3) | async-done | bytes 3145760 | tf_op jit(solution)/shard_map/all_to_all | solution.py:95
  305.5 5.6 copy.71
  311.1 6.3 reshape.137
  317.5 5.3 fusion.17
  322.8 6.7 multiply_convert_fusion.3
  334.0 6.0 convolution_convert_fusion
  342.9 5.8 copy.75
  358.6 33.2 %all-to-all-done.6 = bf16[8,32,6,1024]{3,1,2,0:T(8,128)(2,1)S(1)} async-done(((bf16[8,32,6,1024]{3,1,2,0:T(8,128)(2,1)}), bf16[8,32,6,1024]{3,1,2,0:T(8,128)(2,1)S(1)}, u32[]{:S(2)}, u32[]{:S(2)}) %all-to-all-start.6) | async-done | bytes 3145760 | tf_op jit(solution)/shard_map/all_to_all | solution.py:126
  391.9 7.8 all-to-all-start.9
  408.3 7.0 all-to-all-start.7
  422.4 301.6 %all-reduce.4.cloned.1.call-done = f32[3,1024,512]{1,2,0:T(8,128)} async-done(((f32[3,1024,512]{1,2,0:T(8,128)}), f32[3,1024,512]{1,2,0:T(8,128)}) %all-reduce.4.cloned.1.call-update) | async-done | bytes 6291472 | tf_op jit(solution)/shard_map/psum | solution.py:147
  740.0 8.2 %gather_fusion.4 = bf16[1280]{0:T(1024)(128)(2,1)S(1)} fusion(bf16[1536]{0:T(1024)(128)(2,1)S(1)} %reshape.142, s32[2048]{0:T(1024)S(1)} %pad_clamp_fusion), kind=kCustom, calls=%fused_computation.4 | custom fusion | bytes 10240 | tf_op jit(solution)/shard_map/gather | solution.py:142
  752.9 4.9 reshape.141
  757.7 5.1 gather_fusion.3
  762.9 6.3 reshape.199
  769.2 5.5 reduce_sum.38
  (99 shorter events, 82.8 us)
Async XLA Ops:
  7.2 41.4 %copy-start.4 = (bf16[128,1024]{1,0:T(8,128)(2,1)S(1)}, bf16[128,1024]{1,0:T(8,128)(2,1)}, u32[]{:S(2)}) copy-start(bf16[128,1024]{1,0:T(8,128)(2,1)} %param.6) | copy-start | bytes 786436
  36.9 25.3 %all-to-all-start.1 = ((bf16[8,32,6]{2,0,1:T(8,128)(2,1)}), bf16[8,32,6]{2,0,1:T(8,128)(2,1)S(1)}, u32[]{:S(2)}, u32[]{:S(2)}) async-start(bf16[8,32,6]{2,0,1:T(8,128)(2,1)} %copy.66), calls=%async_computation.1 | async-start | bytes 131072 | tf_op jit(solution)/shard_map/all_to_all | solution.py:102
  62.2 42.0 %all-to-all-start.4 = ((bf16[8,32,6,1024]{3,1,2,0:T(8,128)(2,1)}), bf16[8,32,6,1024]{3,1,2,0:T(8,128)(2,1)S(1)}, u32[]{:S(2)}, u32[]{:S(2)}) async-start(bf16[8,32,6,1024]{3,1,2,0:T(8,128)(2,1)} %copy.72), calls=%async_computation.4 | async-start | bytes 6291456 | tf_op jit(solution)/shard_map/all_to_all | solution.py:89
  104.2 42.9 %all-to-all-start.2 = ((bf16[8,32,6,1024]{3,1,2,0:T(8,128)(2,1)}), bf16[8,32,6,1024]{3,1,2,0:T(8,128)(2,1)}, u32[]{:S(2)}, u32[]{:S(2)}) async-start(bf16[8,32,6,1024]{3,1,2,0:T(8,128)(2,1)} %copy.69), calls=%async_computation.2 | async-start | bytes 6291456 | tf_op jit(solution)/shard_map/all_to_all | solution.py:96
  147.1 80.6 %all-to-all-start.5 = ((bf16[8,32,6,1024]{3,0,2,1:T(8,128)(2,1)}), bf16[8,32,6,1024]{3,0,2,1:T(8,128)(2,1)S(1)}, u32[]{:S(2)}, u32[]{:S(2)}) async-start(bf16[8,32,6,1024]{3,0,2,1:T(8,128)(2,1)} %copy.73), calls=%async_computation.5 | async-start | bytes 6291456 | tf_op jit(solution)/shard_map/all_to_all | solution.py:88
  227.6 77.9 %all-to-all-start.3 = ((bf16[8,32,6,1024]{3,0,2,1:T(8,128)(2,1)}), bf16[8,32,6,1024]{3,0,2,1:T(8,128)(2,1)}, u32[]{:S(2)}, u32[]{:S(2)}) async-start(bf16[8,32,6,1024]{3,0,2,1:T(8,128)(2,1)} %copy.70), calls=%async_computation.3 | async-start | bytes 6291456 | tf_op jit(solution)/shard_map/all_to_all | solution.py:95
  247.3 70.2 %copy-start = (bf16[1536,1024]{1,0:T(8,128)(2,1)}, bf16[1536,1024]{1,0:T(8,128)(2,1)S(1)}, u32[]{:S(2)}) copy-start(bf16[1536,1024]{1,0:T(8,128)(2,1)S(1)} %reshape.139) | copy-start | bytes 9437188
  317.5 5.4 copy-start.2
  322.8 6.7 copy-start.15
  330.5 18.2 %all-to-all-start.8 = ((bf16[8,32,6]{1,2,0:T(8,128)(2,1)}), bf16[8,32,6]{1,2,0:T(8,128)(2,1)S(1)}, u32[]{:S(2)}, u32[]{:S(2)}) async-start(bf16[8,32,6]{1,2,0:T(8,128)(2,1)} %copy.80), calls=%async_computation.8 | async-start | bytes 32768 | tf_op jit(solution)/shard_map/all_to_all | solution.py:133
  348.7 43.2 %all-to-all-start.6 = ((bf16[8,32,6,1024]{3,1,2,0:T(8,128)(2,1)}), bf16[8,32,6,1024]{3,1,2,0:T(8,128)(2,1)S(1)}, u32[]{:S(2)}, u32[]{:S(2)}) async-start(bf16[8,32,6,1024]{3,1,2,0:T(8,128)(2,1)} %copy.75), calls=%async_computation.6 | async-start | bytes 6291456 | tf_op jit(solution)/shard_map/all_to_all | solution.py:126
  353.4 3.1 copy-start.5
  355.2 1.0 copy-start.7
  355.2 1.4 copy-start.9
  391.9 16.5 %all-to-all-start.9 = ((bf16[8,32,6]{2,0,1:T(8,128)(2,1)}), bf16[8,32,6]{2,0,1:T(8,128)(2,1)S(1)}, u32[]{:S(2)}, u32[]{:S(2)}) async-start(bf16[8,32,6]{2,0,1:T(8,128)(2,1)} %copy.81), calls=%async_computation.9 | async-start | bytes 131072 | tf_op jit(solution)/shard_map/all_to_all | solution.py:132
  408.3 340.7 %all-to-all-start.7 = ((bf16[8,32,6,1024]{3,0,2,1:T(8,128)(2,1)}), bf16[8,32,6,1024]{3,0,2,1:T(8,128)(2,1)S(1)}, u32[]{:S(2)}, u32[]{:S(2)}) async-start(bf16[8,32,6,1024]{3,0,2,1:T(8,128)(2,1)} %copy.76), calls=%async_computation.7 | async-start | bytes 6291456 | tf_op jit(solution)/shard_map/all_to_all | solution.py:125
  415.4 308.6 %all-reduce.4.cloned.1.call-start = ((), (), s32[]{:S(2)}) async-start(), calls=%async_computation.10 | async-start | bytes 12582912 | tf_op jit(solution)/shard_map/psum | solution.py:147
  415.6 2.8 copy-start.6
  415.6 2.8 copy-start.11
  728.4 4.4 copy-start.1
  728.4 4.4 copy-start.14
  728.4 6.2 slice-start
  732.8 2.1 copy-start.3
  732.8 2.6 slice-start.1
  769.2 5.6 copy-start.8
  769.2 5.6 copy-start.10
  769.2 5.6 copy-start.12
  769.2 5.6 copy-start.13
Sparse Core Ops, SparseCore 0:
  422.2 301.7 all-reduce.3
where the time goes:
time: 794 us; the launch traced here: 784 us
  waiting for transfers between devices  516 us (65%)
  local copies, waits for them, and re-layouts  134 us (17%)
  starting transfers between devices  60.4 us (8%)
  matrix products  35.2 us (4%)
  between operations  15 us (2%)
  other arithmetic  13.6 us (2%)
  blocking collectives  9.64 us (1%)
    psum x1, waiting for transfers between devices, shards(): summed = lax.psum(local_terms, ('dp', 'expert'))  302 us
    all_to_all x1, waiting for transfers between devices, shards(): lax.all_to_all(lax.all_to_all(send_tokens, 'dp', split_axis=0, concat_axi...  65.4 us
    all_to_all x1, waiting for transfers between devices, shards(): lax.all_to_all(lax.all_to_all(send_cotangent, 'dp', split_axis=0, concat_...  58.2 us
    all_to_all x1, waiting for transfers between devices, shards(): lax.all_to_all(send_cotangent, 'dp', split_axis=0, concat_axis=0, tiled=T...  35 us
    all_to_all x1, waiting for transfers between devices, shards(): lax.all_to_all(outgoing_input, 'dp', split_axis=0, concat_axis=0, tiled=T...  33.2 us
    all_to_all x1, waiting for transfers between devices, shards(): lax.all_to_all(send_tokens, 'dp', split_axis=0, concat_axis=0, tiled=True)  19.6 us
  transfers between devices with their start and end apart: 10, of which 7 were waited for; matrix products, arithmetic and copies ran while one was open for 14% of the time, Pallas kernels for 0%

commit v1 on v0

v1 whole, which is shorter than its diff:
```python
import functools

import jax
import jax.numpy as jnp
from jax import lax
from jax.experimental import pallas as pl
from jax.experimental.pallas import tpu as pltpu
from jax.sharding import PartitionSpec as P

MESH = pl.DeviceIdType.MESH
BF = jnp.bfloat16
F32 = jnp.float32
NY, NC, NX, NZ = 4, 2, 4, 8
NPL = NY * NC * NX
CAP = 6
CH = 16
NCH = NZ * CAP // CH
SEQ = (0, 1, 7, 2, 6, 3, 5, 4)
POS = {j: q for q, j in enumerate(SEQ)}
BLOCKS = tuple((c * CH // CAP, -(-(c + 1) * CH // CAP)) for c in range(NCH))
ORDER = tuple(
    (i * 8 + c * 4 + (i + j) % 4) for j in range(4) for c in range(2) for i in range(4)
)
ORDER = tuple(o for o in ORDER if o)


def coords():
    d = lax.axis_index("dp")
    e = lax.axis_index("expert")
    return d // 2, d % 2, e % 4, e // 4


def plane_peer(o, sign=1):
    y, c, x, z = coords()
    dy, dc, dx = o // 8, (o // 4) % 2, o % 4
    return (
        lax.rem(y + sign * dy + NY, NY) * 2 + lax.rem(c + dc, NC),
        z * NX + lax.rem(x + sign * dx + NX, NX),
    )


def z_peer(j):
    y, c, x, z = coords()
    return (y * 2 + c, lax.rem(z + j + NZ, NZ) * NX + x)


def greet():
    bar = pltpu.get_barrier_semaphore()
    for o in range(1, NPL):
        pl.semaphore_signal(bar, inc=1, device_id=plane_peer(o), device_id_type=MESH)
    for j in range(1, NZ):
        pl.semaphore_signal(bar, inc=1, device_id=z_peer(j), device_id_type=MESH)
    pl.semaphore_wait(bar, NPL - 1 + NZ - 1)


def remote(src, dst, ss, rs, dev):
    return pltpu.make_async_remote_copy(
        src_ref=src, dst_ref=dst, send_sem=ss, recv_sem=rs, device_id=dev, device_id_type=MESH
    )


def pick(rank, chunk, q):
    rows = lax.broadcasted_iota(jnp.int32, (NPL, CH, 128), 1) + (chunk * CH - q * CAP)
    return jnp.broadcast_to(rank[:, None, :], (NPL, CH, 128)) == rows.astype(F32)


def dispatch_kernel(
    x_ref, y_ref, rg_ref, rx, ry, xg, yg, rgo, sx, sy, px, pg, zs, zr, ms, mr, cs, cr
):
    greet()
    metas = []
    for j in range(1, NZ):
        cp = remote(rg_ref.at[j], rgo.at[POS[j]], ms.at[j], mr.at[j], z_peer(j))
        cp.start()
        metas.append(cp)
    rgo[0] = rg_ref[0]

    def ring(j_from, j_to, k, src):
        dst = (xg, yg)[k]
        step = 1 if (j_to - j_from) % NZ == 1 else -1
        i = POS[j_to] * 2 + k
        return remote(src, dst.at[POS[j_to]], zs.at[i], zr.at[i], z_peer(step))

    cps = {}

    def go(j_from, j_to, k):
        src = (x_ref, y_ref)[k] if j_from == 0 else (xg, yg)[k].at[POS[j_from]]
        cps[(j_to, k)] = ring(j_from, j_to, k, src)
        cps[(j_to, k)].start()

    for k in range(2):
        go(0, 1, k)
        go(0, 7, k)
    xg[0] = x_ref[...]
    yg[0] = y_ref[...]
    for m in metas:
        m.wait()

    outs = []

    def pack(chunk):
        q0, q1 = BLOCKS[chunk]
        width = (q1 - q0) * 128
        for q in range(q0, q1):
            rank = rgo[q, 0:NPL, :].astype(F32)
            gate = rgo[q, NPL : 2 * NPL, :].astype(F32)
            hit = pick(rank, chunk, q)
            lanes = slice((q - q0) * 128, (q - q0 + 1) * 128)
            px[:, lanes] = jnp.where(hit, 1.0, 0.0).astype(BF).reshape(NPL * CH, 128)
            gates = jnp.broadcast_to(gate[:, None, :], (NPL, CH, 128))
            pg[:, lanes] = jnp.where(hit, gates, 0.0).astype(BF).reshape(NPL * CH, 128)

        def group(g, carry):
            rows = pl.ds(pl.multiple_of(g * 128, 128), 128)
            for sel, blk, out in ((px, xg, sx), (pg, yg, sy)):
                data = blk[q0:q1].reshape(width, blk.shape[2])
                got = jnp.dot(sel[rows, 0:width], data, preferred_element_type=F32)
                out[chunk, pl.ds(pl.multiple_of(g * 8, 8), 8)] = got.astype(BF).reshape(
                    8, CH, blk.shape[2]
                )
            return carry

        lax.fori_loop(0, NPL // 8, group, 0)
        rx[chunk, 0] = sx[chunk, 0]
        ry[chunk, 0] = sy[chunk, 0]
        for o in ORDER:
            for k, (s, r) in enumerate(((sx, rx), (sy, ry))):
                cp = remote(
                    s.at[chunk, o],
                    r.at[chunk, o],
                    cs.at[k, chunk, o],
                    cr.at[k, chunk, o],
                    plane_peer(o),
                )
                cp.start()
                outs.append(cp)

    def arrived(*keys):
        for key in keys:
            cps[key].wait_recv()

    for k in range(2):
        arrived((1, k))
        go(1, 2, k)
        arrived((7, k))
        go(7, 6, k)
    pack(0)
    for k in range(2):
        arrived((2, k))
        go(2, 3, k)
        arrived((6, k))
        go(6, 5, k)
    arrived((3, 0))
    go(3, 4, 0)
    arrived((5, 1))
    go(5, 4, 1)
    arrived((3, 1), (5, 0))
    pack(1)
    arrived((4, 0), (4, 1))
    pack(2)
    for key in cps:
        cps[key].wait_send()
    for cp in outs:
        cp.wait()


def dispatch(x, y, rg):
    t, d = x.shape
    vm = pl.BlockSpec(memory_space=pltpu.VMEM)
    rows = jax.ShapeDtypeStruct((NCH, NPL, CH, d), BF)
    return pl.pallas_call(
        dispatch_kernel,
        out_shape=(
            rows,
            rows,
            jax.ShapeDtypeStruct((NZ, t, d), BF),
            jax.ShapeDtypeStruct((NZ, t, d), BF),
            jax.ShapeDtypeStruct((NZ, 2 * NPL, t), BF),
        ),
        in_specs=[vm] * 3,
        out_specs=(vm,) * 5,
        scratch_shapes=[
            pltpu.VMEM((NCH, NPL, CH, d), BF),
            pltpu.VMEM((NCH, NPL, CH, d), BF),
            pltpu.VMEM((NPL * CH, 4 * 128), BF),
            pltpu.VMEM((NPL * CH, 4 * 128), BF),
            pltpu.SemaphoreType.DMA((2 * NZ,)),
            pltpu.SemaphoreType.DMA((2 * NZ,)),
            pltpu.SemaphoreType.DMA((NZ,)),
            pltpu.SemaphoreType.DMA((NZ,)),
            pltpu.SemaphoreType.DMA((2, NCH, NPL)),
            pltpu.SemaphoreType.DMA((2, NCH, NPL)),
        ],
        compiler_params=pltpu.CompilerParams(
            collective_id=0, has_side_effects=True, vmem_limit_bytes=60 << 20
        ),
        name="dispatch",
    )(x, y, rg)


def collect_kernel(
    dx_ref, gs_ref, rg_ref, sp_ref, gsh_ref,
    out, dgo, sho, ret, gsr, zsend, zrecv, dsend, sh1, sh2,
    cs, cr, gss, gsrs, zs, zr, ds, dr, s1s, s1r, s2s, s2r, s3s, s3r,
):
    y, c, x, z = coords()
    greet()
    sends = []

    def start(cp):
        cp.start()
        sends.append(cp)
        return cp

    dps = [o for o in range(0, NPL, 4)]
    part1 = []
    for i, o in enumerate(dps):
        if o == 0:
            continue
        dev = plane_peer(o)
        src = gsh_ref.at[:, pl.ds(pl.multiple_of(dev[0] * 128, 128), 128)]
        part1.append(start(remote(src, sh1.at[i], s1s.at[i], s1r.at[i], dev)))
    gates = []
    for o in ORDER:
        gates.append(
            start(remote(gs_ref.at[o], gsr.at[o], gss.at[o], gsrs.at[o], plane_peer(o, -1)))
        )
    gsr[0] = gs_ref[0]
    rows = []
    for chunk in range(NCH):
        got = []
        for o in ORDER:
            got.append(
                start(
                    remote(
                        dx_ref.at[chunk, o],
                        ret.at[chunk, o],
                        cs.at[chunk, o],
                        cr.at[chunk, o],
                        plane_peer(o, -1),
                    )
                )
            )
        ret[chunk, 0] = dx_ref[chunk, 0]
        rows.append(got)

    for cp in part1:
        cp.wait_recv()
    mine = pl.ds(pl.multiple_of((y * 2 + c) * 128, 128), 128)
    total = gsh_ref[:, mine]
    for i in range(1, len(dps)):
        total = total + sh1[i]
    sh2[0] = total
    part2 = []
    for o in (1, 3, 2):
        part2.append(start(remote(sh2.at[0], sh2.at[o], s2s.at[o], s2r.at[o], plane_peer(o))))
    for cp in part2:
        cp.wait_recv()
    sho[z] = sh2[0] + sh2[1] + sh2[2] + sh2[3]
    part3 = []
    for j in (1, 7, 2, 6, 3, 5, 4):
        part3.append(start(remote(sho.at[z], sho.at[z], s3s.at[j], s3r.at[j], z_peer(j))))

    for cp in gates:
        cp.wait_recv()
    lane = lax.broadcasted_iota(jnp.int32, (NPL, CH, 128), 2)
    row = lax.broadcasted_iota(jnp.int32, (NPL, CH, 128), 1)
    zgot = []
    done = 0
    for chunk in range(NCH):
        for cp in rows[chunk]:
            cp.wait_recv()
        q0, q1 = BLOCKS[chunk]
        spread = jnp.broadcast_to(gsr[:, 0, :][:, None, :], (NPL, CH, 128))
        value = jnp.sum(
            jnp.where(lane == row + chunk * CH, spread, 0.0), axis=2, keepdims=True
        )
        for q in range(q0, q1):
            rank = rg_ref[q, 0:NPL, :].astype(F32)
            hit = pick(rank, chunk, q)
            sel = jnp.where(hit, 1.0, 0.0).astype(BF).reshape(NPL * CH, 128)
            dterm = jnp.sum(jnp.where(hit, value, 0.0), axis=1)
            part = lax.dot_general(
                sel,
                ret[chunk].reshape(NPL * CH, ret.shape[3]),
                (((0,), (0,)), ((), ())),
                preferred_element_type=F32,
            )
            if q * CAP < chunk * CH:
                sp_ref[q] = sp_ref[q] + part
                dsend[q] = dsend[q] + dterm
            else:
                sp_ref[q] = sp_ref[q] + part
                dsend[q] = dterm
            if (q + 1) * CAP <= (chunk + 1) * CH and q > 0:
                j = SEQ[q]
                zsend[q] = sp_ref[q].astype(BF)
                zgot.append(start(remote(zsend.at[q], zrecv.at[q], zs.at[q], zr.at[q], z_peer(-j))))
                zgot.append(start(remote(dsend.at[q], dgo.at[j], ds.at[q], dr.at[q], z_peer(-j))))
    dgo[0] = dsend[0]
    for cp in zgot:
        cp.wait_recv()
    acc = sp_ref[0]
    for q in range(1, NZ):
        acc = acc + zrecv[q].astype(F32)
    out[...] = acc.astype(BF)
    for cp in part3:
        cp.wait_recv()
    for cp in sends:
        cp.wait_send()


def collect(dx, gs, rg, sp, gsh):
    d = dx.shape[-1]
    t = rg.shape[-1]
    n3 = gsh.shape[0]
    vm = pl.BlockSpec(memory_space=pltpu.VMEM)
    dma = pltpu.SemaphoreType.DMA

    def body(dx_ref, gs_ref, rg_ref, sp_ref, gsh_ref, out, dgo, sho, acc, *rest):
        acc[...] = sp_ref[...]
        collect_kernel(dx_ref, gs_ref, rg_ref, acc, gsh_ref, out, dgo, sho, *rest)

    return pl.pallas_call(
        body,
        out_shape=(
            jax.ShapeDtypeStruct((t, d), BF),
            jax.ShapeDtypeStruct((NZ, NPL, t), F32),
            jax.ShapeDtypeStruct((NZ, n3, 128), F32),
        ),
        in_specs=[vm] * 5,
        out_specs=(vm,) * 3,
        scratch_shapes=[
            pltpu.VMEM((NZ, t, d), F32),
            pltpu.VMEM((NCH, NPL, CH, d), BF),
            pltpu.VMEM((NPL, 1, 128), F32),
            pltpu.VMEM((NZ, t, d), BF),
            pltpu.VMEM((NZ, t, d), BF),
            pltpu.VMEM((NZ, NPL, t), F32),
            pltpu.VMEM((8, n3, 128), F32),
            pltpu.VMEM((4, n3, 128), F32),
            dma((NCH, NPL)), dma((NCH, NPL)),
            dma((NPL,)), dma((NPL,)),
            dma((NZ,)), dma((NZ,)), dma((NZ,)), dma((NZ,)),
            dma((8,)), dma((8,)), dma((4,)), dma((4,)), dma((NZ,)), dma((NZ,)),
        ],
        compiler_params=pltpu.CompilerParams(
            collective_id=1, has_side_effects=True, vmem_limit_bytes=60 << 20
        ),
        name="collect",
    )(dx, gs, rg, sp, gsh)


def silu_parts(pre):
    sigma = jax.nn.sigmoid(pre)
    return (pre * sigma, sigma * (1.0 + pre * (1.0 - sigma)))


def dot(a, b, dims):
    return lax.dot_general(a, b, ((dims[0], dims[1]), ((), ())), preferred_element_type=F32)


def units(x, gy, weight):
    pre_gate = dot(x, weight[0], ((1,), (0,)))
    pre_up = dot(x, weight[1], ((1,), (0,)))
    back = dot(gy, weight[2], ((1,), (0,)))
    activated, slope = silu_parts(pre_gate)
    hidden = activated * pre_up
    gate_grad = jnp.sum(hidden * back, axis=1)
    ggi = (back * pre_up * slope).astype(BF)
    gui = (back * activated).astype(BF)
    return ggi, gui, hidden.astype(BF), gate_grad


def shards(tokens, cotangent, expert_ids, gate_weights, expert_weights, shared_weights):
    t, d = tokens.shape
    y, c, x, z = coords()
    r = jnp.arange(NZ * NPL, dtype=jnp.int32)
    j, o = r // NPL, r % NPL
    dy, dc, dx = o // 8, (o // 4) % 2, o % 4
    owner = (((y + dy) % NY) * 2 + (c + dc) % NC) * (NZ * NX) + ((z + j) % NZ) * NX + (x + dx) % NX
    match = expert_ids.T[:, None, :] == owner[None, :, None]
    named = jnp.any(match, axis=0)
    gate = jnp.sum(jnp.where(match, gate_weights.astype(F32).T[:, None, :], 0.0), axis=0)
    ids = jnp.arange(t, dtype=jnp.int32)
    earlier = (ids[:, None] < ids[None, :]).astype(BF)
    rank = jnp.dot(named.astype(BF), earlier, preferred_element_type=F32)
    rank = jnp.where(named, rank, -100.0)
    rg = jnp.concatenate(
        [rank.astype(BF).reshape(NZ, NPL, t), gate.astype(BF).reshape(NZ, NPL, t)], axis=1
    )
    rx, ry, xg, yg, rgo = dispatch(tokens, cotangent, rg)

    slots = NCH * NPL * CH
    w = expert_weights[0]
    ex, ey = rx.reshape(slots, d), ry.reshape(slots, d)
    ggi, gui, hid, gate_grad = units(ex, ey, w)
    dxr = dot(ggi, w[0], ((1,), (1,))) + dot(gui, w[1], ((1,), (1,)))
    dxr = dxr.astype(BF).reshape(NCH, NPL, CH, d)
    gs = gate_grad.reshape(NCH, NPL, CH).transpose(1, 0, 2).reshape(NPL, 1, NCH * CH)
    gs = jnp.pad(gs, ((0, 0), (0, 0), (0, 128 - NCH * CH)))

    f = shared_weights.shape[2] // NZ
    sw = lax.dynamic_slice_in_dim(shared_weights, z * f, f, 2)
    sx, sy = xg.reshape(NZ * t, d), yg.reshape(NZ * t, d)
    sggi, sgui, shid, _ = units(sx, sy, sw)
    sp = dot(sggi, sw[0], ((1,), (1,))) + dot(sgui, sw[1], ((1,), (1,)))
    gsh = jnp.concatenate(
        [
            dot(sggi, sx, ((0,), (0,))),
            dot(sgui, sx, ((0,), (0,))),
            dot(shid, sy, ((0,), (0,))),
        ],
        axis=0,
    )
    grad_tokens, dg, sh = collect(dxr, gs, rgo, sp.reshape(NZ, t, d), gsh)

    grad_experts = jnp.stack(
        [
            dot(ex, ggi, ((0,), (0,))),
            dot(ex, gui, ((0,), (0,))),
            dot(ey, hid, ((0,), (0,))),
        ],
        axis=0,
    ).astype(BF)[None]
    dgr = dg.reshape(NZ * NPL, t)
    picked = jnp.sum(jnp.where(match, dgr[None], 0.0), axis=1)
    grad_gates = (picked.T / gate_weights.astype(F32)).astype(BF)
    grad_shared = sh.reshape(NZ, 3, f, 128).transpose(1, 3, 0, 2).reshape(3, 128, NZ * f)
    return (grad_tokens, grad_gates, grad_experts, grad_shared)


def solution(mesh):
    rows = P(("dp", "expert"), None)
    return jax.shard_map(
        shards,
        mesh=mesh,
        in_specs=(rows, rows, rows, rows, P(("dp", "expert"), None, None, None), P()),
        out_specs=(rows, rows, P(("dp", "expert"), None, None, None), P(None, "dp", None)),
        check_vma=False,
    )
```

time: 794 us -> 280 us (0.35); the launches traced: 784 us -> 279 us
  waiting for transfers between devices: 516 us -> 0 us
  Pallas kernels: 0 us -> 229 us
  local copies, waits for them, and re-layouts: 134 us -> 8.03 us
  starting transfers between devices: 60.4 us -> 0 us
  between operations: 15 us -> 0.95 us
  blocking collectives: 9.64 us -> 0 us
    psum x1 -> x0, waiting for transfers between devices: 302 us -> none  [shards(): summed = lax.psum(local_terms, ('dp', 'expert'))]
    pallas_call x0 -> x2, Pallas kernels: none -> 229 us  [the longest x1 123 us: collect(): pl.pallas_call(body, out_shape=(jax.ShapeDtypeStruct((t, d), BF), jax.Sha...]
    all_to_all x9 -> x0, waiting for transfers between devices: 214 us -> none  [the longest x1 65.4 us: shards(): lax.all_to_all(lax.all_to_all(send_tokens, 'dp', split_axis=0, concat_axi...]
    all_to_all x9 -> x0, starting transfers between devices: 60.1 us -> none  [the longest x1 11.6 us: shards(): lax.all_to_all(lax.all_to_all(send_gates, 'dp', split_axis=0, concat_axis...]
    reshape x14 -> x3, local copies, waits for them, and re-layouts: 46 us -> 2.25 us  [the longest x1 2.1 us: shards(): sh.reshape(NZ, 3, f, 128).transpose(1, 3, 0, 2).reshape(3, 128, NZ * f)]
    gather x6 -> x0, local copies, waits for them, and re-layouts: 33.9 us -> none  [the longest x1 9.46 us: shards(): padded_gates[slot_table].reshape(data_count, expert_count, capacity)]
    all_to_all x10 -> x0, local copies, waits for them, and re-layouts: 27.1 us -> none  [the longest x1 5.64 us: shards(): lax.all_to_all(lax.all_to_all(send_cotangent, 'dp', split_axis=0, concat_...]
    all_to_all x1 -> x0, blocking collectives: 9.64 us -> none  [shards(): lax.all_to_all(send_gates, 'dp', split_axis=0, concat_axis=0, tiled=True)]
  transfers between devices with their start and end apart: 10 -> 0, of which waited for: 7 -> 0; matrix products, arithmetic and copies ran while one was open for 14% -> 0% of each run, Pallas kernels for 0% -> 0%
where the time goes in v1:
time: 280 us; the launch traced here: 279 us
  Pallas kernels  229 us (82%)
  matrix products  32.8 us (12%)
  other arithmetic  8.1 us (3%)
  local copies, waits for them, and re-layouts  8.03 us (3%)
    pallas_call x1, Pallas kernels, collect(): pl.pallas_call(body, out_shape=(jax.ShapeDtypeStruct((t, d), BF), jax.Sha...  123 us
    pallas_call x1, Pallas kernels, dispatch(): pl.pallas_call(dispatch_kernel, out_shape=(rows, rows, jax.ShapeDtypeStru...  106 us
    dot_general x16, matrix products, dot(): lax.dot_general(a, b, ((dims[0], dims[1]), ((), ())), preferred_element_t...  32.6 us

profile of v1, /device:TPU:2, one launch (start us, length us, event | category | flops | bytes accessed | tf_op | source)
XLA Modules:
  0.0 279.0 jit_solution(919081643782165687)
XLA Ops:
  0.7 0.8 convert_bitcast_fusion
  1.6 1.0 compare_reduce_fusion
  2.7 0.9 fusion.12
  3.6 0.7 pad_maximum_fusion.2.rg_ref
  4.3 106.3 %dispatch.1 = (bf16[3,32,16,1024]{3,2,1,0:T(8,128)(2,1)}, bf16[3,32,16,1024]{3,2,1,0:T(8,128)(2,1)}, bf16[8,128,1024]{2,1,0:T(8,128)(2,1)}, bf16[8,128,1024]{2,1,0:T(8,128)(2,1)}, bf16[8,64,128]{2,1,0:T(8,128)(2,1)}) custom-call(bf16[128,1024]{1,0:T(8,128)(2,1)} %x_ref.1, bf16[128,1024]{1,0:T(8,128)(2,1)} %y_ref.1, bf16[8,64,128]{2,1,0:T(8,128)(2,1)} %pad_maximum_fusion.2.rg_ref), custom_call_target="tpu_custom_call" | custom-call | tf_op jit(solution)/shard_map/dispatch/pallas_call | solution.py:171
  110.6 2.6 fusion.32
  113.2 0.8 fusion.33
  114.0 0.9 multiply_convert_fusion.3
  114.9 0.5 fusion.34
  115.4 0.5 fusion.59
  115.8 0.5 fusion.58
  116.3 0.9 pad_maximum_fusion.1.gsh_ref
  117.3 1.2 copy-done.10
  118.5 1.9 fusion.17
  120.4 1.9 fusion.20
  122.3 3.0 %fusion.7 = bf16[1,1,1024,512]{3,2,1,0:T(8,128)(2,1)} fusion(bf16[1536,1024]{1,0:T(8,128)(2,1)S(1)} %bitcast.97, f32[1536,512]{0,1:T(8,128)S(1)} %fusion.20, f32[1536,512]{0,1:T(8,128)S(1)} %fusion.17), kind=kOutput, calls=%fused_computation.17 | convolution fusion | flops 1615855616 | bytes 10485760 | tf_op jit(solution)/shard_map/dot_general | solution.py:360
  125.3 4.8 %multiply_reduce_fusion = (f32[1536]{0:T(1024)S(1)}, bf16[1536,512]{0,1:T(8,128)(2,1)}, bf16[1536,512]{0,1:T(8,128)(2,1)}) fusion(f32[1536,512]{0,1:T(8,128)S(1)} %fusion.20, f32[1536,512]{0,1:T(8,128)S(1)} %fusion.17, bf16[1536,1024]{1,0:T(8,128)(2,1)S(1)} %bitcast.98, bf16[1,3,1024,512]{3,2,1,0:T(8,128)(2,1)S(1)} %copy-done.5), kind=kOutput, calls=%fused_computation.2 | convolution fusion | flops 1623194112 | bytes 13637632 | tf_op jit(solution)/shard_map/dot_general | solution.py:360
  130.3 0.6 pad.4.gs_ref
  131.0 4.3 %fusion.10 = bf16[1,1,1024,512]{3,2,1,0:T(8,128)(2,1)S(1)} fusion(bf16[1536,1024]{1,0:T(8,128)(2,1)} %bitcast.93, bf16[1536,512]{0,1:T(8,128)(2,1)} %get-tuple-element.29), kind=kOutput, calls=%fused_computation.18 | convolution fusion | flops 1611137024 | bytes 5767168 | tf_op jit(solution)/shard_map/dot_general | solution.py:360
  135.3 1.9 fusion.11
  137.2 2.0 pad_maximum_fusion
  139.2 0.8 fusion.31
  140.0 2.9 %convolution_add_fusion = f32[1024,1024]{1,0:T(8,128)} fusion(f32[1024,1024]{1,0:T(8,128)S(1)} %fusion.31, bf16[1024,64]{0,1:T(8,128)(2,1)S(1)} %get-tuple-element.31, bf16[3,1024,512]{2,1,0:T(8,128)(2,1)S(1)} %copy-done, s32[]{:T(128)S(6)} %add.198, s32[]{:T(128)S(6)} %select_n.134), kind=kOutput, calls=%fused_computation.7 | convolution fusion | flops 135266304 | bytes 8781832 | tf_op jit(solution)/shard_map/dot_general | solution.py:360
  143.0 0.8 copy-done.13
  143.8 1.8 fusion.15
  145.6 3.6 %add_convert_fusion = bf16[1536,1024]{1,0:T(8,128)(2,1)} fusion(f32[1536,1024]{1,0:T(8,128)S(1)} %fusion.15, bf16[1536,512]{0,1:T(8,128)(2,1)S(1)} %copy-done.3, bf16[1,3,1024,512]{3,2,1,0:T(8,128)(2,1)S(1)} %copy-done.6), kind=kOutput, calls=%fused_computation | convolution fusion | flops 1613758464 | bytes 12058624 | tf_op jit(solution)/shard_map/dot_general | solution.py:360
  149.3 122.9 %collect.1 = (bf16[128,1024]{1,0:T(8,128)(2,1)}, f32[8,32,128]{2,1,0:T(8,128)}, f32[8,192,128]{2,1,0:T(8,128)}) custom-call(bf16[3,32,16,1024]{3,2,1,0:T(8,128)(2,1)} %bitcast.80, f32[32,1,128]{2,1,0:T(1,128)} %pad.4.gs_ref, bf16[8,64,128]{2,1,0:T(8,128)(2,1)} %get-tuple-element.14.rg_ref, f32[8,128,1024]{2,1,0:T(8,128)} %bitcast.79, ...), custom_call_target="tpu_custom_call" | custom-call | tf_op jit(solution)/shard_map/collect/pallas_call | solution.py:324
  272.2 1.1 fusion.13
  273.4 0.6 fusion.36
  274.0 2.1 copy.17
  276.1 2.3 copy.18
  278.3 0.7 copy.20
  (31 shorter events, 0.5 us)
Async XLA Ops:
  0.6 109.9 %copy-start = (bf16[3,1024,512]{2,1,0:T(8,128)(2,1)S(1)}, bf16[3,1024,512]{2,1,0:T(8,128)(2,1)}, u32[]{:S(2)}) copy-start(bf16[3,1024,512]{2,1,0:T(8,128)(2,1)} %param.11) | copy-start | bytes 9437188
  110.5 2.6 copy-start.1
  110.6 3.4 %copy-start.2 = (bf16[8,128,1024]{2,1,0:T(8,128)(2,1)S(1)}, bf16[8,128,1024]{2,1,0:T(8,128)(2,1)}, u32[]{:S(2)}) copy-start(bf16[8,128,1024]{2,1,0:T(8,128)(2,1)} %get-tuple-element.15) | copy-start | bytes 6291460
  115.3 1.9 copy-start.5
  115.3 3.1 %copy-start.10 = (bf16[3,32,16,1024]{3,2,1,0:T(8,128)(2,1)S(1)}, bf16[3,32,16,1024]{3,2,1,0:T(8,128)(2,1)}, u32[]{:S(2)}) copy-start(bf16[3,32,16,1024]{3,2,1,0:T(8,128)(2,1)} %get-tuple-element.13) | copy-start | bytes 9437188
  120.4 1.9 copy-start.12
  130.9 4.4 %copy-start.3 = (bf16[1536,512]{0,1:T(8,128)(2,1)S(1)}, bf16[1536,512]{0,1:T(8,128)(2,1)}, u32[]{:S(2)}) copy-start(bf16[1536,512]{0,1:T(8,128)(2,1)} %get-tuple-element.30) | copy-start | bytes 4718596
  131.0 4.4 %copy-start.11 = (bf16[3,32,16,1024]{3,2,1,0:T(8,128)(2,1)S(1)}, bf16[3,32,16,1024]{3,2,1,0:T(8,128)(2,1)}, u32[]{:S(2)}) copy-start(bf16[3,32,16,1024]{3,2,1,0:T(8,128)(2,1)} %get-tuple-element.13) | copy-start | bytes 9437188
  135.3 1.9 copy-start.4
  140.0 2.9 %copy-start.6 = (bf16[1,3,1024,512]{3,2,1,0:T(8,128)(2,1)S(1)}, bf16[1,3,1024,512]{3,2,1,0:T(8,128)(2,1)}, u32[]{:S(2)}) copy-start(bf16[1,3,1024,512]{3,2,1,0:T(8,128)(2,1)} %param.10) | copy-start | bytes 9437188
  140.0 3.8 %copy-start.13 = (bf16[1536,512]{0,1:T(8,128)(2,1)S(1)}, bf16[1536,512]{0,1:T(8,128)(2,1)}, u32[]{:S(2)}) copy-start(bf16[1536,512]{0,1:T(8,128)(2,1)} %get-tuple-element.29) | copy-start | bytes 4718596
  149.3 122.9 %copy-start.8 = (s32[128,10]{0,1:T(8,128)S(1)}, s32[128,10]{0,1:T(8,128)}, u32[]{:S(2)}) copy-start(s32[128,10]{0,1:T(8,128)} %param.8) | copy-start | bytes 15364
  149.3 124.1 %copy-start.9 = (bf16[128,10]{0,1:T(8,128)(2,1)S(1)}, bf16[128,10]{0,1:T(8,128)(2,1)}, u32[]{:S(2)}) copy-start(bf16[128,10]{0,1:T(8,128)(2,1)} %param.9) | copy-start | bytes 7684
  272.2 6.2 %copy-start.7 = (bf16[128,1024]{1,0:T(8,128)(2,1)S(1)}, bf16[128,1024]{1,0:T(8,128)(2,1)}, u32[]{:S(2)}) copy-start(bf16[128,1024]{1,0:T(8,128)(2,1)} %get-tuple-element.37) | copy-start | bytes 786436

commit v2 on v1

v2 whole, which is shorter than its diff:
```python
import functools

import jax
import jax.numpy as jnp
from jax import lax
from jax.experimental import pallas as pl
from jax.experimental.pallas import tpu as pltpu
from jax.sharding import PartitionSpec as P

MESH = pl.DeviceIdType.MESH
BF = jnp.bfloat16
F32 = jnp.float32
NY, NC, NX, NZ = 4, 2, 4, 8
NPL = NY * NC * NX
CAP = 6
CH = 16
NCH = NZ * CAP // CH
SEQ = (0, 1, 7, 2, 6, 3, 5, 4)
POS = {j: q for q, j in enumerate(SEQ)}
BLOCKS = tuple((c * CH // CAP, -(-(c + 1) * CH // CAP)) for c in range(NCH))
ORDER = tuple(
    (i * 8 + c * 4 + (i + j) % 4) for j in range(4) for c in range(2) for i in range(4)
)
ORDER = tuple(o for o in ORDER if o)


def coords():
    d = lax.axis_index("dp")
    e = lax.axis_index("expert")
    return d // 2, d % 2, e % 4, e // 4


def plane_peer(o, sign=1):
    y, c, x, z = coords()
    dy, dc, dx = o // 8, (o // 4) % 2, o % 4
    return (
        lax.rem(y + sign * dy + NY, NY) * 2 + lax.rem(c + dc, NC),
        z * NX + lax.rem(x + sign * dx + NX, NX),
    )


def z_peer(j):
    y, c, x, z = coords()
    return (y * 2 + c, lax.rem(z + j + NZ, NZ) * NX + x)


def greet():
    bar = pltpu.get_barrier_semaphore()
    for o in range(1, NPL):
        pl.semaphore_signal(bar, inc=1, device_id=plane_peer(o), device_id_type=MESH)
    for j in range(1, NZ):
        pl.semaphore_signal(bar, inc=1, device_id=z_peer(j), device_id_type=MESH)
    pl.semaphore_wait(bar, NPL - 1 + NZ - 1)


def remote(src, dst, ss, rs, dev):
    return pltpu.make_async_remote_copy(
        src_ref=src, dst_ref=dst, send_sem=ss, recv_sem=rs, device_id=dev, device_id_type=MESH
    )


def pick(rank, chunk, q):
    rows = lax.broadcasted_iota(jnp.int32, (NPL, CH, 128), 1) + (chunk * CH - q * CAP)
    return jnp.broadcast_to(rank[:, None, :], (NPL, CH, 128)) == rows.astype(F32)


def dot(a, b, ca, cb):
    return lax.dot_general(a, b, (((ca,), (cb,)), ((), ())), preferred_element_type=F32)


def units(pre_gate, pre_up, back):
    sigma = jax.nn.sigmoid(pre_gate)
    activated = pre_gate * sigma
    slope = sigma * (1.0 + pre_gate * (1.0 - sigma))
    hidden = activated * pre_up
    ggi = (back * pre_up * slope).astype(BF)
    gui = (back * activated).astype(BF)
    return ggi, gui, hidden


def layer_kernel(
    x_ref, y_ref, rg_ref, w_hbm, sw_ref,
    out, dgo, ge, gsho,
    w, rx, ry, xg, yg, rgo, sx, sy, px, pg,
    ggi, gui, hid, dxr, ret, gs, gsr, acc, gsh, gshb, sh1, sh2, sh3, zout, zin, dsend,
    wsem, zs, zr, ms, mr, cs, cr, bs, br, gss, grs, us, ur, ds, dr, s1s, s1r, s2s, s2r, s3s, s3r,
):
    y, c, x, z = coords()
    d = x_ref.shape[1]
    f = w.shape[2]
    sends = []

    def start(cp):
        cp.start()
        sends.append(cp)
        return cp

    load = pltpu.make_async_copy(w_hbm.at[0], w, wsem)
    load.start()
    greet()

    metas = []
    for j in range(1, NZ):
        metas.append(
            start(remote(rg_ref.at[j], rgo.at[POS[j]], ms.at[j], mr.at[j], z_peer(j)))
        )
    rgo[0] = rg_ref[0]

    cps = {}

    def go(j_from, j_to, k):
        src = (x_ref, y_ref)[k] if j_from == 0 else (xg, yg)[k].at[POS[j_from]]
        step = 1 if (j_to - j_from) % NZ == 1 else -1
        i = POS[j_to] * 2 + k
        dst = (xg, yg)[k].at[POS[j_to]]
        cps[(j_to, k)] = start(remote(src, dst, zs.at[i], zr.at[i], z_peer(step)))

    def arrived(*keys):
        for key in keys:
            cps[key].wait_recv()

    for k in range(2):
        go(0, 1, k)
        go(0, 7, k)
    xg[0] = x_ref[...]
    yg[0] = y_ref[...]
    for m in metas:
        m.wait_recv()

    rows_in = {}

    def pack(chunk):
        q0, q1 = BLOCKS[chunk]
        width = (q1 - q0) * 128
        for q in range(q0, q1):
            rank = rgo[q, 0:NPL, :].astype(F32)
            gate = rgo[q, NPL : 2 * NPL, :].astype(F32)
            hit = pick(rank, chunk, q)
            lanes = slice((q - q0) * 128, (q - q0 + 1) * 128)
            px[:, lanes] = jnp.where(hit, 1.0, 0.0).astype(BF).reshape(NPL * CH, 128)
            gates = jnp.broadcast_to(gate[:, None, :], (NPL, CH, 128))
            pg[:, lanes] = jnp.where(hit, gates, 0.0).astype(BF).reshape(NPL * CH, 128)

        def group(g, carry):
            rows = pl.ds(pl.multiple_of(g * 128, 128), 128)
            for sel, blk, dst in ((px, xg, sx), (pg, yg, sy)):
                data = blk[q0:q1].reshape(width, d)
                got = dot(sel[rows, 0:width], data, 1, 0)
                dst[chunk, pl.ds(pl.multiple_of(g * 8, 8), 8)] = got.astype(BF).reshape(8, CH, d)
            return carry

        lax.fori_loop(0, NPL // 8, group, 0)
        rx[chunk, 0] = sx[chunk, 0]
        ry[chunk, 0] = sy[chunk, 0]
        got = []
        for o in ORDER:
            for k, (s, r) in enumerate(((sx, rx), (sy, ry))):
                sem = (k, chunk, o)
                got.append(
                    start(
                        remote(
                            s.at[chunk, o], r.at[chunk, o], cs.at[sem], cr.at[sem], plane_peer(o)
                        )
                    )
                )
        rows_in[chunk] = got

    for k in range(2):
        arrived((1, k))
        go(1, 2, k)
        arrived((7, k))
        go(7, 6, k)
    pack(0)
    for k in range(2):
        arrived((2, k))
        go(2, 3, k)
        arrived((6, k))
        go(6, 5, k)
    arrived((3, 0))
    go(3, 4, 0)
    arrived((5, 1))
    go(5, 4, 1)
    arrived((3, 1), (5, 0))
    pack(1)
    arrived((4, 0), (4, 1))
    pack(2)

    gsh[...] = jnp.zeros_like(gsh)

    def shared(g, carry):
        two = pl.ds(pl.multiple_of(g * 2, 2), 2)
        bx = xg[two].reshape(256, d)
        by = yg[two].reshape(256, d)
        a, b, hidden = units(
            dot(bx, sw_ref[0], 1, 0), dot(bx, sw_ref[1], 1, 0), dot(by, sw_ref[2], 1, 0)
        )
        n = sw_ref.shape[2]
        acc[two] = (dot(a, sw_ref[0], 1, 1) + dot(b, sw_ref[1], 1, 1)).reshape(2, 128, d)
        gsh[0:n, :] += dot(a, bx, 0, 0)
        gsh[n : 2 * n, :] += dot(b, bx, 0, 0)
        gsh[2 * n : 3 * n, :] += dot(hidden.astype(BF), by, 0, 0)
        return carry

    lax.fori_loop(0, NZ // 2, shared, 0)
    gshb[...] = gsh[...].astype(BF)
    part1 = []
    for i in range(1, 8):
        dev = plane_peer(i * 4)
        src = gshb.at[:, pl.ds(pl.multiple_of(dev[0] * 128, 128), 128)]
        part1.append(start(remote(src, sh1.at[i], s1s.at[i], s1r.at[i], dev)))
    load.wait()

    lane3 = lax.broadcasted_iota(jnp.int32, (16, CH, 128), 2)
    row3 = lax.broadcasted_iota(jnp.int32, (16, CH, 128), 1)

    def expert(chunk):
        for cp in rows_in[chunk]:
            cp.wait_recv()

        def group(g, carry):
            os = pl.ds(pl.multiple_of(g * 16, 16), 16)
            rs = pl.ds(pl.multiple_of(chunk * 512 + g * 256, 256), 256)
            bx = rx[chunk, os].reshape(256, d)
            by = ry[chunk, os].reshape(256, d)
            back = dot(by, w[2], 1, 0)
            a, b, hidden = units(dot(bx, w[0], 1, 0), dot(bx, w[1], 1, 0), back)
            ggi[rs, :] = a
            gui[rs, :] = b
            hid[rs, :] = hidden.astype(BF)
            gg = jnp.sum(hidden * back, axis=1, keepdims=True).reshape(16, CH, 1)
            term = jnp.where(lane3 == row3 + chunk * CH, gg, 0.0)
            term = jnp.sum(term, axis=1, keepdims=True)
            if chunk == 0:
                gs[os] = term
            else:
                gs[os] = gs[os] + term
            grads = dot(a, w[0], 1, 1) + dot(b, w[1], 1, 1)
            dxr[chunk, os] = grads.astype(BF).reshape(16, CH, d)
            return carry

        lax.fori_loop(0, 2, group, 0)

    rows_back = {}

    def give_back(chunk):
        got = []
        for o in ORDER:
            sem = (chunk, o)
            got.append(
                start(
                    remote(
                        dxr.at[chunk, o], ret.at[chunk, o], bs.at[sem], br.at[sem],
                        plane_peer(o, -1),
                    )
                )
            )
        ret[chunk, 0] = dxr[chunk, 0]
        rows_back[chunk] = got

    expert(0)
    expert(1)
    give_back(1)
    expert(2)
    give_back(2)
    give_back(0)
    gates = []
    for o in ORDER:
        gates.append(start(remote(gs.at[o], gsr.at[o], gss.at[o], grs.at[o], plane_peer(o, -1))))
    gsr[0] = gs[0]

    for cp in part1:
        cp.wait_recv()
    mine = pl.ds(pl.multiple_of((y * 2 + c) * 128, 128), 128)
    total = gsh[:, mine]
    for i in range(1, 8):
        total = total + sh1[i].astype(F32)
    sh2[0] = total.astype(BF)
    part2 = []
    for o in (1, 3, 2):
        part2.append(start(remote(sh2.at[0], sh2.at[o], s2s.at[o], s2r.at[o], plane_peer(o))))

    def wgrad(g, carry):
        cols = pl.ds(pl.multiple_of(g * 256, 256), 256)
        bx = rx[:, :, :, cols].reshape(NCH * NPL * CH, 256)
        ge[0, cols, :] = dot(bx, ggi[...], 0, 0).astype(BF)
        ge[1, cols, :] = dot(bx, gui[...], 0, 0).astype(BF)
        by = ry[:, :, :, cols].reshape(NCH * NPL * CH, 256)
        ge[2, cols, :] = dot(by, hid[...], 0, 0).astype(BF)
        return carry

    lax.fori_loop(0, d // 256, wgrad, 0)

    for cp in part2:
        cp.wait_recv()
    total = sh2[0].astype(F32)
    for o in range(1, 4):
        total = total + sh2[o].astype(F32)
    sh3[z] = total.astype(BF)
    part3 = []
    for j in (1, 7, 2, 6, 3, 5, 4):
        part3.append(start(remote(sh3.at[z], sh3.at[z], s3s.at[j], s3r.at[j], z_peer(j))))

    lane = lax.broadcasted_iota(jnp.int32, (NPL, CH, 128), 2)
    row = lax.broadcasted_iota(jnp.int32, (NPL, CH, 128), 1)
    for cp in gates:
        cp.wait_recv()
    seen = set()
    left = {q: sum(b0 <= q < b1 for b0, b1 in BLOCKS) for q in range(NZ)}
    dgot = []

    def combine(chunk):
        for cp in rows_back[chunk]:
            cp.wait_recv()
        spread = jnp.broadcast_to(gsr[...], (NPL, CH, 128))
        value = jnp.sum(jnp.where(lane == row + chunk * CH, spread, 0.0), axis=2, keepdims=True)
        for q in reversed(range(*BLOCKS[chunk])):
            hit = pick(rgo[q, 0:NPL, :].astype(F32), chunk, q)
            sel = jnp.where(hit, 1.0, 0.0).astype(BF).reshape(NPL * CH, 128)
            acc[q] = acc[q] + dot(sel, ret[chunk].reshape(NPL * CH, d), 0, 0)
            dterm = jnp.sum(jnp.where(hit, value, 0.0), axis=1)
            dsend[q] = dsend[q] + dterm if q in seen else dterm
            seen.add(q)
            left[q] -= 1
            if not left[q] and q:
                j = SEQ[q]
                dgot.append(start(remote(dsend.at[q], dgo.at[j], ds.at[q], dr.at[q], z_peer(-j))))

    ring = {}

    def pass_on(j):
        lo = slice(0, d // 2)
        hi = slice(d // 2, d)
        q = POS[j]
        if j == 4:
            zout[4] = acc[q].astype(BF)
            ring[3] = start(
                remote(zout.at[4, :, lo], zin.at[3, :, lo], us.at[3], ur.at[3], z_peer(-1))
            )
            ring[5] = start(
                remote(zout.at[4, :, hi], zin.at[5, :, hi], us.at[5], ur.at[5], z_peer(1))
            )
            return
        ring[j].wait_recv()
        part = {3: lo, 5: hi}.get(j, slice(0, d))
        acc[q, :, part] = acc[q, :, part] + zin[j, :, part].astype(F32)
        zout[j] = acc[q].astype(BF)
        if j < 4:
            to, dev = j - 1, z_peer(-1)
        else:
            to, dev = (j + 1) % NZ or 4, z_peer(1)
        ring[to] = start(remote(zout.at[j], zin.at[to], us.at[to], ur.at[to], dev))

    combine(1)
    combine(2)
    for j in (4, 5, 3, 6, 2):
        pass_on(j)
    combine(0)
    for j in (7, 1):
        pass_on(j)
    dgo[0] = dsend[0]
    for cp in part3:
        cp.wait_recv()
    n = sw_ref.shape[2]
    for k in range(3):
        for m in range(NZ // 2):
            pair = [sh3[2 * m + i, k * n : (k + 1) * n, :].astype(F32) for i in range(2)]
            gsho[k, :, m * 2 * n : (m + 1) * 2 * n] = jnp.concatenate(pair, axis=0).T
    for cp in dgot:
        cp.wait_recv()
    ring[4].wait_recv()
    ring[0].wait_recv()
    out[...] = (acc[0] + zin[0].astype(F32) + zin[4].astype(F32)).astype(BF)
    for cp in sends:
        cp.wait_send()


def layer(xs, ys, rg, weights, sw):
    t, d = xs.shape
    f = weights.shape[3]
    n = sw.shape[2]
    slots = NCH * NPL * CH
    vm = pl.BlockSpec(memory_space=pltpu.VMEM)
    hbm = pl.BlockSpec(memory_space=pl.ANY)
    dma = pltpu.SemaphoreType.DMA
    v = pltpu.VMEM
    return pl.pallas_call(
        layer_kernel,
        out_shape=(
            jax.ShapeDtypeStruct((t, d), BF),
            jax.ShapeDtypeStruct((NZ, NPL, t), F32),
            jax.ShapeDtypeStruct((3, d, f), BF),
            jax.ShapeDtypeStruct((3, 128, NZ * n), F32),
        ),
        in_specs=[vm, vm, vm, hbm, vm],
        out_specs=(vm,) * 4,
        scratch_shapes=[
            v((3, d, f), BF),
            v((NCH, NPL, CH, d), BF), v((NCH, NPL, CH, d), BF),
            v((NZ, t, d), BF), v((NZ, t, d), BF), v((NZ, 2 * NPL, t), BF),
            v((NCH, NPL, CH, d), BF), v((NCH, NPL, CH, d), BF),
            v((NPL * CH, 512), BF), v((NPL * CH, 512), BF),
            v((slots, f), BF), v((slots, f), BF), v((slots, f), BF),
            v((NCH, NPL, CH, d), BF), v((NCH, NPL, CH, d), BF),
            v((NPL, 1, 128), F32), v((NPL, 1, 128), F32),
            v((NZ, t, d), F32),
            v((3 * n, d), F32), v((3 * n, d), BF),
            v((8, 3 * n, 128), BF), v((4, 3 * n, 128), BF), v((NZ, 3 * n, 128), BF),
            v((NZ, t, d), BF), v((NZ, t, d), BF),
            v((NZ, NPL, t), F32),
            dma,
            dma((2 * NZ,)), dma((2 * NZ,)), dma((NZ,)), dma((NZ,)),
            dma((2, NCH, NPL)), dma((2, NCH, NPL)), dma((NCH, NPL)), dma((NCH, NPL)),
            dma((NPL,)), dma((NPL,)), dma((NZ,)), dma((NZ,)), dma((NZ,)), dma((NZ,)),
            dma((8,)), dma((8,)), dma((4,)), dma((4,)), dma((NZ,)), dma((NZ,)),
        ],
        compiler_params=pltpu.CompilerParams(
            collective_id=0, has_side_effects=True, vmem_limit_bytes=61 << 20
        ),
        name="layer",
    )(xs, ys, rg, weights, sw)


def shards(tokens, cotangent, expert_ids, gate_weights, expert_weights, shared_weights):
    t, d = tokens.shape
    y, c, x, z = coords()
    r = jnp.arange(NZ * NPL, dtype=jnp.int32)
    j, o = r // NPL, r % NPL
    dy, dc, dx = o // 8, (o // 4) % 2, o % 4
    owner = (((y + dy) % NY) * 2 + (c + dc) % NC) * (NZ * NX) + ((z + j) % NZ) * NX + (x + dx) % NX
    match = expert_ids.T[:, None, :] == owner[None, :, None]
    named = jnp.any(match, axis=0)
    gate = jnp.sum(jnp.where(match, gate_weights.astype(F32).T[:, None, :], 0.0), axis=0)
    ids = jnp.arange(t, dtype=jnp.int32)
    earlier = (ids[:, None] < ids[None, :]).astype(BF)
    rank = jnp.dot(named.astype(BF), earlier, preferred_element_type=F32)
    rank = jnp.where(named, rank, -100.0)
    rg = jnp.concatenate(
        [rank.astype(BF).reshape(NZ, NPL, t), gate.astype(BF).reshape(NZ, NPL, t)], axis=1
    )
    f = shared_weights.shape[2] // NZ
    sw = lax.dynamic_slice_in_dim(shared_weights, z * f, f, 2)
    grad_tokens, dg, ge, grad_shared = layer(tokens, cotangent, rg, expert_weights, sw)
    dgr = dg.reshape(NZ * NPL, t)
    picked = jnp.sum(jnp.where(match, dgr[None], 0.0), axis=1)
    grad_gates = (picked.T / gate_weights.astype(F32)).astype(BF)
    return (grad_tokens, grad_gates, ge[None], grad_shared)


def solution(mesh):
    rows = P(("dp", "expert"), None)
    return jax.shard_map(
        shards,
        mesh=mesh,
        in_specs=(rows, rows, rows, rows, P(("dp", "expert"), None, None, None), P()),
        out_specs=(rows, rows, P(("dp", "expert"), None, None, None), P(None, "dp", None)),
        check_vma=False,
    )
```

time: 280 us -> 197 us (0.70)
  Pallas kernels: 229 us -> 181 us
  matrix products: 32.8 us -> 0.16 us
  other arithmetic: 8.1 us -> 4.92 us
    pallas_call x2 -> x1, Pallas kernels: 229 us -> 181 us  [layer(): pl.pallas_call(layer_kernel, out_shape=(jax.ShapeDtypeStruct((t, d), BF),...]
    dot_general x16 -> x0, matrix products: 32.6 us -> none  [dot(): lax.dot_general(a, b, ((dims[0], dims[1]), ((), ())), preferred_element_t...]
    unnamed x30 -> x9, local copies, waits for them, and re-layouts: 5.08 us -> 6.39 us
where the time goes in v2:
time: 197 us; the launch traced here: 195 us
  Pallas kernels  181 us (92%)
  local copies, waits for them, and re-layouts  8.68 us (4%)
  other arithmetic  4.92 us (2%)
    pallas_call x1, Pallas kernels, layer(): pl.pallas_call(layer_kernel, out_shape=(jax.ShapeDtypeStruct((t, d), BF),...  181 us
    unnamed x9, local copies, waits for them, and re-layouts  6.39 us

profile of v2, /device:TPU:2, one launch (start us, length us, event | category | flops | bytes accessed | tf_op | source)
XLA Modules:
  0.0 195.1 jit_solution(12335537657843832410)
XLA Ops:
  0.7 0.7 convert_bitcast_fusion
  1.4 0.9 compare_reduce_fusion
  2.3 0.2 fusion.2
  2.5 0.9 fusion
  3.4 0.7 pad_maximum_fusion.rg_ref
  4.1 2.3 %constant_dynamic-slice_fusion.sw_ref = bf16[3,1024,64]{2,1,0:T(8,128)(2,1)} fusion(bf16[3,1024,512]{2,1,0:T(8,128)(2,1)} %param.11, s32[]{:T(128)S(6)} %select_n.134), kind=kLoop, calls=%fused_computation.54 | loop fusion | bytes 786436 | tf_op jit(solution)/shard_map/dynamic_slice | solution.py:441
  6.3 0.0 copy-start.1
  6.3 0.0 copy-start.2
  6.3 180.7 %layer.1 = (bf16[128,1024]{1,0:T(8,128)(2,1)}, f32[8,32,128]{2,1,0:T(8,128)}, bf16[3,1024,512]{2,1,0:T(8,128)(2,1)}, f32[3,128,512]{2,1,0:T(8,128)}) custom-call(bf16[128,1024]{1,0:T(8,128)(2,1)} %x_ref.1, bf16[128,1024]{1,0:T(8,128)(2,1)} %y_ref.1, bf16[8,64,128]{2,1,0:T(8,128)(2,1)} %pad_maximum_fusion.rg_ref, bf16[1,3,1024,512]{3,2,1,0:T(8,128)(2,1)} %w_hbm.1, ...), custom_call_target="tpu_custom_call" | custom-call | tf_op jit(solution)/shard_map/layer/pallas_call | solution.py:386
  187.0 0.0 copy-done.1
  187.0 1.1 fusion.1
  188.1 0.0 copy-done.2
  188.1 0.6 fusion.3
  188.7 1.7 copy.13
  190.4 0.0 copy-start
  190.4 3.8 %copy.14 = bf16[1,3,1024,512]{3,2,1,0:T(8,128)(2,1)} copy(bf16[1,3,1024,512]{3,2,1,0:T(8,128)(2,1)} %bitcast.10) | data formatting | bytes 6291456
  194.2 0.0 copy-done
  194.3 0.9 copy.15
  (1 shorter events, 0.0 us)
Async XLA Ops:
  6.3 180.7 %copy-start.1 = (s32[128,10]{0,1:T(8,128)S(1)}, s32[128,10]{0,1:T(8,128)}, u32[]{:S(2)}) copy-start(s32[128,10]{0,1:T(8,128)} %param.8) | copy-start | bytes 15364
  6.3 181.8 %copy-start.2 = (bf16[128,10]{0,1:T(8,128)(2,1)S(1)}, bf16[128,10]{0,1:T(8,128)(2,1)}, u32[]{:S(2)}) copy-start(bf16[128,10]{0,1:T(8,128)(2,1)} %param.9) | copy-start | bytes 7684
  190.4 3.8 %copy-start = (f32[3,128,512]{2,1,0:T(8,128)S(1)}, f32[3,128,512]{2,1,0:T(8,128)}, u32[]{:S(2)}) copy-start(f32[3,128,512]{2,1,0:T(8,128)} %get-tuple-element.19) | copy-start | bytes 2359300

commit v3 on v2

v3 whole, which is shorter than its diff:
```python
import jax
import jax.numpy as jnp
from jax import lax
from jax.experimental import pallas as pl
from jax.experimental.pallas import tpu as pltpu
from jax.sharding import PartitionSpec as P

MESH = pl.DeviceIdType.MESH
BF = jnp.bfloat16
F32 = jnp.float32
NY, NC, NX, NZ = 4, 2, 4, 8
NPL = NY * NC * NX
CAP = 6
CH = 16
NCH = NZ * CAP // CH
SEQ = (0, 1, 7, 2, 6, 3, 5, 4)
POS = {j: q for q, j in enumerate(SEQ)}
BLOCKS = tuple((c * CH // CAP, -(-(c + 1) * CH // CAP)) for c in range(NCH))
ORDER = tuple(
    (i * 8 + c * 4 + (i + j) % 4) for j in range(4) for c in range(2) for i in range(4)
)
ORDER = tuple(o for o in ORDER if o)


def coords():
    d = lax.axis_index("dp")
    e = lax.axis_index("expert")
    return d // 2, d % 2, e % 4, e // 4


def plane_peer(o, sign=1):
    y, c, x, z = coords()
    dy, dc, dx = o // 8, (o // 4) % 2, o % 4
    return (
        lax.rem(y + sign * dy + NY, NY) * 2 + lax.rem(c + dc, NC),
        z * NX + lax.rem(x + sign * dx + NX, NX),
    )


def z_peer(j):
    y, c, x, z = coords()
    return (y * 2 + c, lax.rem(z + j + NZ, NZ) * NX + x)


def owners(j):
    y, c, x, z = coords()
    o = lax.broadcasted_iota(jnp.int32, (NPL, 128), 0)
    dp = lax.rem(y + (o >> 3), NY) * 2 + lax.rem(c + ((o >> 2) & 1), NC)
    return dp * (NZ * NX) + lax.rem(z + j, NZ) * NX + lax.rem(x + (o & 3), NX)


def greet():
    bar = pltpu.get_barrier_semaphore()
    for o in range(1, NPL):
        pl.semaphore_signal(bar, inc=1, device_id=plane_peer(o), device_id_type=MESH)
    for j in range(1, NZ):
        pl.semaphore_signal(bar, inc=1, device_id=z_peer(j), device_id_type=MESH)


def greeted():
    pl.semaphore_wait(pltpu.get_barrier_semaphore(), NPL - 1 + NZ - 1)


def remote(src, dst, ss, rs, dev):
    return pltpu.make_async_remote_copy(
        src_ref=src, dst_ref=dst, send_sem=ss, recv_sem=rs, device_id=dev, device_id_type=MESH
    )


def pick(rank, chunk, q):
    rows = lax.broadcasted_iota(jnp.int32, (NPL, CH, 128), 1) + (chunk * CH - q * CAP)
    return jnp.broadcast_to(rank[:, None, :], (NPL, CH, 128)) == rows.astype(F32)


def dot(a, b, ca, cb):
    return lax.dot_general(a, b, (((ca,), (cb,)), ((), ())), preferred_element_type=F32)


def units(pre_gate, pre_up, back):
    sigma = jax.nn.sigmoid(pre_gate)
    activated = pre_gate * sigma
    slope = sigma * (1.0 + pre_gate * (1.0 - sigma))
    hidden = activated * pre_up
    ggi = (back * pre_up * slope).astype(BF)
    gui = (back * activated).astype(BF)
    return ggi, gui, hidden


def layer_kernel(
    x_hbm, y_hbm, ids_ref, gw_ref, w_hbm, sw_hbm,
    out, ggo, ge_hbm, gs_hbm,
    w, swb, sw_ref, ge, gsho, rg_ref, dgo, rx, ry, xg, yg, rgo, sx, sy, px, pg,
    ggi, gui, hid, dxr, ret, gs, gsr, acc, gsh, gshb, sh1, sh2, sh3, zout, zin, dsend,
    wsem, xsem, ysem, ssem, gsem, fsem, zs, zr, ms, mr, cs, cr, bs, br, gss, grs, us, ur, ds, dr, s1s, s1r, s2s, s2r, s3s, s3r,
):
    y, c, x, z = coords()
    d = x_hbm.shape[1]
    sends = []

    def start(cp):
        cp.start()
        sends.append(cp)
        return cp

    greet()
    own = (
        pltpu.make_async_copy(x_hbm, xg.at[0], xsem),
        pltpu.make_async_copy(y_hbm, yg.at[0], ysem),
    )
    load = pltpu.make_async_copy(w_hbm.at[0], w, wsem)
    halves = pl.ds(pl.multiple_of((z // 2) * 128, 128), 128)
    loads = pltpu.make_async_copy(sw_hbm.at[:, :, halves], swb, ssem)
    own[0].start()
    own[1].start()
    loads.start()
    load.start()
    older = lax.broadcasted_iota(jnp.int32, (128, 128), 0)
    earlier = (older < lax.broadcasted_iota(jnp.int32, (128, 128), 1)).astype(F32).astype(BF)
    for j in range(NZ):
        who = owners(j)
        named = jnp.zeros((NPL, 128), F32)
        gate = jnp.zeros((NPL, 128), F32)
        for k in range(ids_ref.shape[0]):
            hit = ids_ref[k : k + 1, :] == who
            named = jnp.where(hit, 1.0, named)
            gate = jnp.where(hit, gw_ref[k : k + 1, :].astype(F32), gate)
        rank = dot(named.astype(BF), earlier, 1, 0)
        rg_ref[j, 0:NPL, :] = jnp.where(named > 0.5, rank, -100.0).astype(BF)
        rg_ref[j, NPL : 2 * NPL, :] = gate.astype(BF)
    own[0].wait()
    own[1].wait()
    greeted()

    cps = {}

    def go(j_from, j_to, k):
        src = (xg, yg)[k].at[POS[j_from]]
        step = 1 if (j_to - j_from) % NZ == 1 else -1
        i = POS[j_to] * 2 + k
        dst = (xg, yg)[k].at[POS[j_to]]
        cps[(j_to, k)] = start(remote(src, dst, zs.at[i], zr.at[i], z_peer(step)))

    def arrived(*keys):
        for key in keys:
            cps[key].wait_recv()

    metas = []
    for j in range(1, NZ):
        metas.append(
            start(remote(rg_ref.at[j], rgo.at[POS[j]], ms.at[j], mr.at[j], z_peer(j)))
        )
    for k in range(2):
        go(0, 1, k)
        go(0, 7, k)
    rgo[0] = rg_ref[0]

    for m in metas:
        m.wait_recv()

    rows_in = {chunk: [] for chunk in range(NCH)}

    def pack(chunk, k):
        q0, q1 = BLOCKS[chunk]
        width = (q1 - q0) * 128
        sel, blk, snd, rcv = ((px, xg, sx, rx), (pg, yg, sy, ry))[k]
        for q in range(q0, q1):
            hit = pick(rgo[q, 0:NPL, :].astype(F32), chunk, q)
            if k:
                gate = rgo[q, NPL : 2 * NPL, :].astype(F32)
                value = jnp.broadcast_to(gate[:, None, :], (NPL, CH, 128))
            else:
                value = 1.0
            lanes = slice((q - q0) * 128, (q - q0 + 1) * 128)
            sel[:, lanes] = jnp.where(hit, value, 0.0).astype(BF).reshape(NPL * CH, 128)

        def group(g, carry):
            rows = pl.ds(pl.multiple_of(g * 256, 256), 256)
            got = dot(sel[rows, 0:width], blk[q0:q1].reshape(width, d), 1, 0)
            os = pl.ds(pl.multiple_of(g * 16, 16), 16)
            snd[chunk, os] = got.astype(BF).reshape(16, CH, d)
            return carry

        lax.fori_loop(0, NPL // 16, group, 0)
        rcv[chunk, 0] = snd[chunk, 0]
        for o in ORDER:
            sem = (k, chunk, o)
            rows_in[chunk].append(
                start(
                    remote(
                        snd.at[chunk, o], rcv.at[chunk, o], cs.at[sem], cr.at[sem], plane_peer(o)
                    )
                )
            )

    def forward(j_from, j_to, k):
        arrived((j_from, k))
        go(j_from, j_to, k)

    for k in range(2):
        forward(1, 2, k)
        forward(7, 6, k)
        pack(0, k)
    for k in range(2):
        forward(2, 3, k)
        forward(6, 5, k)
    forward(3, 4, 0)
    arrived((5, 0))
    pack(1, 0)
    forward(5, 4, 1)
    arrived((3, 1))
    pack(1, 1)
    arrived((4, 0))
    pack(2, 0)
    arrived((4, 1))
    pack(2, 1)

    loads.wait()
    n = swb.shape[2] // 2
    sw_ref[...] = jnp.where(lax.rem(z, 2) == 1, swb[:, :, n:], swb[:, :, :n])
    gsh[...] = jnp.zeros_like(gsh)

    def shared(g, carry):
        two = pl.ds(pl.multiple_of(g * 2, 2), 2)
        bx = xg[two].reshape(256, d)
        by = yg[two].reshape(256, d)
        a, b, hidden = units(
            dot(bx, sw_ref[0], 1, 0), dot(bx, sw_ref[1], 1, 0), dot(by, sw_ref[2], 1, 0)
        )
        n = sw_ref.shape[2]
        acc[two] = (dot(a, sw_ref[0], 1, 1) + dot(b, sw_ref[1], 1, 1)).reshape(2, 128, d)
        gsh[0:n, :] += dot(a, bx, 0, 0)
        gsh[n : 2 * n, :] += dot(b, bx, 0, 0)
        gsh[2 * n : 3 * n, :] += dot(hidden.astype(BF), by, 0, 0)
        return carry

    lax.fori_loop(0, NZ // 2, shared, 0)
    gshb[...] = gsh[...].astype(BF)
    part1 = []
    for i in range(1, 8):
        dev = plane_peer(i * 4)
        src = gshb.at[:, pl.ds(pl.multiple_of(dev[0] * 128, 128), 128)]
        part1.append(start(remote(src, sh1.at[i], s1s.at[i], s1r.at[i], dev)))
    load.wait()

    lane3 = lax.broadcasted_iota(jnp.int32, (16, CH, 128), 2)
    row3 = lax.broadcasted_iota(jnp.int32, (16, CH, 128), 1)

    def expert(chunk):
        for cp in rows_in[chunk]:
            cp.wait_recv()

        def group(g, carry):
            os = pl.ds(pl.multiple_of(g * 16, 16), 16)
            rs = pl.ds(pl.multiple_of(chunk * 512 + g * 256, 256), 256)
            bx = rx[chunk, os].reshape(256, d)
            by = ry[chunk, os].reshape(256, d)
            back = dot(by, w[2], 1, 0)
            a, b, hidden = units(dot(bx, w[0], 1, 0), dot(bx, w[1], 1, 0), back)
            ggi[rs, :] = a
            gui[rs, :] = b
            hid[rs, :] = hidden.astype(BF)
            gg = jnp.sum(hidden * back, axis=1, keepdims=True).reshape(16, CH, 1)
            term = jnp.where(lane3 == row3 + chunk * CH, gg, 0.0)
            term = jnp.sum(term, axis=1, keepdims=True)
            if chunk == 0:
                gs[os] = term
            else:
                gs[os] = gs[os] + term
            grads = dot(a, w[0], 1, 1) + dot(b, w[1], 1, 1)
            dxr[chunk, os] = grads.astype(BF).reshape(16, CH, d)
            return carry

        lax.fori_loop(0, 2, group, 0)

    rows_back = {}

    lo = slice(0, d // 2)
    hi = slice(d // 2, d)

    def give_back(chunk, sem, part):
        got = []
        for o in ORDER:
            got.append(
                start(
                    remote(
                        dxr.at[chunk, o, :, part], ret.at[chunk, o, :, part],
                        bs.at[sem, o], br.at[sem, o], plane_peer(o, -1),
                    )
                )
            )
        rows_back[sem] = got

    expert(0)
    expert(1)
    give_back(1, 1, slice(0, d))
    expert(2)
    for cp in part1:
        cp.wait_recv()
    mine = pl.ds(pl.multiple_of((y * 2 + c) * 128, 128), 128)
    total = gsh[:, mine]
    for i in range(1, 8):
        total = total + sh1[i].astype(F32)
    sh2[0] = total.astype(BF)
    part2 = []
    for o in (1, 3, 2):
        part2.append(start(remote(sh2.at[0], sh2.at[o], s2s.at[o], s2r.at[o], plane_peer(o))))
    gates = []
    for o in ORDER:
        gates.append(start(remote(gs.at[o], gsr.at[o], gss.at[o], grs.at[o], plane_peer(o, -1))))
    gsr[0] = gs[0]
    give_back(2, 2, slice(0, d))
    give_back(0, 0, lo)
    give_back(0, NCH, hi)
    for chunk in range(NCH):
        ret[chunk, 0] = dxr[chunk, 0]

    def wgrad(g, carry):
        cols = pl.ds(pl.multiple_of(g * 256, 256), 256)
        bx = rx[:, :, :, cols].reshape(NCH * NPL * CH, 256)
        ge[0, cols, :] = dot(bx, ggi[...], 0, 0).astype(BF)
        ge[1, cols, :] = dot(bx, gui[...], 0, 0).astype(BF)
        by = ry[:, :, :, cols].reshape(NCH * NPL * CH, 256)
        ge[2, cols, :] = dot(by, hid[...], 0, 0).astype(BF)
        return carry

    lax.fori_loop(0, d // 256, wgrad, 0)
    save = pltpu.make_async_copy(ge, ge_hbm, gsem)
    save.start()

    for cp in part2:
        cp.wait_recv()
    total = sh2[0].astype(F32)
    for o in range(1, 4):
        total = total + sh2[o].astype(F32)
    sh3[z] = total.astype(BF)
    part3 = []
    for j in (1, 7, 2, 6, 3, 5, 4):
        part3.append(start(remote(sh3.at[z], sh3.at[z], s3s.at[j], s3r.at[j], z_peer(j))))

    lane = lax.broadcasted_iota(jnp.int32, (NPL, CH, 128), 2)
    row = lax.broadcasted_iota(jnp.int32, (NPL, CH, 128), 1)
    for cp in gates:
        cp.wait_recv()
    seen = set()
    left = {q: sum(b0 <= q < b1 for b0, b1 in BLOCKS) for q in range(NZ)}
    dgot = []

    ring = {}

    def hop(j, to, h):
        part = (lo, hi)[h]
        to = 4 if j == 7 else to
        ring[(to, h)] = start(
            remote(
                zout.at[j, :, part], zin.at[to, :, part], us.at[to, h], ur.at[to, h],
                z_peer(-1) if j in (1, 2, 3) or (j, to) == (4, 3) else z_peer(1),
            )
        )

    def pass_on(j, h):
        part = (lo, hi)[h]
        q = POS[j]
        value = acc[q, :, part]
        if j != 4 and (j, h) not in ((3, 1), (5, 0)):
            ring[(j, h)].wait_recv()
            value = value + zin[j, :, part].astype(F32)
        zout[j, :, part] = value.astype(BF)
        if j == 4:
            hop(j, (3, 5)[h], h)
        elif j < 4:
            hop(j, j - 1, h)
        else:
            hop(j, (j + 1) % NZ, h)

    def gate_terms(chunk):
        spread = jnp.broadcast_to(gsr[...], (NPL, CH, 128))
        value = jnp.sum(jnp.where(lane == row + chunk * CH, spread, 0.0), axis=2, keepdims=True)
        for q in reversed(range(*BLOCKS[chunk])):
            hit = pick(rgo[q, 0:NPL, :].astype(F32), chunk, q)
            i = q - BLOCKS[chunk][0]
            sel = jnp.where(hit, 1.0, 0.0).astype(BF).reshape(NPL * CH, 128)
            px[:, i * 128 : (i + 1) * 128] = sel
            dterm = jnp.sum(jnp.where(hit, value, 0.0), axis=1)
            dsend[q] = dsend[q] + dterm if q in seen else dterm
            seen.add(q)
            left[q] -= 1
            if not left[q] and q:
                j = SEQ[q]
                dgot.append(start(remote(dsend.at[q], dgo.at[j], ds.at[q], dr.at[q], z_peer(-j))))

    def combine(chunk, sem, part, after):
        for cp in rows_back[sem]:
            cp.wait_recv()
        data = ret[chunk, :, :, part].reshape(NPL * CH, part.stop - part.start)
        for q in reversed(range(*BLOCKS[chunk])):
            i = q - BLOCKS[chunk][0]
            sel = px[:, i * 128 : (i + 1) * 128]
            acc[q, :, part] = acc[q, :, part] + dot(sel, data, 0, 0)
            for step in after.get(SEQ[q], ()):
                pass_on(*step)

    full = slice(0, d)
    gate_terms(1)
    combine(1, 1, full, {})
    gate_terms(2)
    combine(2, 2, full, {4: ((4, 0), (4, 1)), 5: ((5, 0),), 3: ((3, 1),)})
    for step in ((3, 0), (5, 1), (2, 1), (6, 0), (2, 0), (6, 1)):
        pass_on(*step)
    gate_terms(0)
    combine(0, 0, lo, {7: ((7, 0),), 1: ((1, 0),)})
    combine(0, NCH, hi, {7: ((7, 1),), 1: ((1, 1),)})
    dgo[0] = dsend[0]
    for cp in part3:
        cp.wait_recv()
    for k in range(3):
        for m in range(NZ // 2):
            pair = [sh3[2 * m + i, k * n : (k + 1) * n, :].astype(F32) for i in range(2)]
            gsho[k, :, m * 2 * n : (m + 1) * 2 * n] = jnp.concatenate(pair, axis=0).T
    save_shared = pltpu.make_async_copy(gsho, gs_hbm, fsem)
    save_shared.start()
    for cp in dgot:
        cp.wait_recv()
    rows = []
    for k in range(ids_ref.shape[0]):
        total = jnp.zeros((NPL, 128), F32)
        for j in range(NZ):
            total = jnp.where(ids_ref[k : k + 1, :] == owners(j), dgo[j], total)
        gate = gw_ref[k : k + 1, :].astype(F32)
        rows.append(jnp.sum(total, axis=0, keepdims=True) / gate)
    ggo[...] = jnp.concatenate(rows, axis=0).astype(BF)
    for h, part in enumerate((lo, hi)):
        ring[(4, h)].wait_recv()
        ring[(0, h)].wait_recv()
        total = acc[0, :, part] + zin[0, :, part].astype(F32) + zin[4, :, part].astype(F32)
        out[:, part] = total.astype(BF)
    save.wait()
    save_shared.wait()
    for cp in sends:
        cp.wait_send()


def layer(xs, ys, ids, gates, weights, shared):
    t, d = xs.shape
    f = weights.shape[3]
    n = shared.shape[2] // NZ
    slots = NCH * NPL * CH
    vm = pl.BlockSpec(memory_space=pltpu.VMEM)
    hbm = pl.BlockSpec(memory_space=pl.ANY)
    dma = pltpu.SemaphoreType.DMA
    v = pltpu.VMEM
    return pl.pallas_call(
        layer_kernel,
        out_shape=(
            jax.ShapeDtypeStruct((t, d), BF),
            jax.ShapeDtypeStruct(gates.shape, BF),
            jax.ShapeDtypeStruct((3, d, f), BF),
            jax.ShapeDtypeStruct((3, 128, NZ * n), F32),
        ),
        in_specs=[hbm, hbm, vm, vm, hbm, hbm],
        out_specs=(vm, vm, hbm, hbm),
        scratch_shapes=[
            v((3, d, f), BF), v((3, d, 2 * n), BF), v((3, d, n), BF), v((3, d, f), BF),
            v((3, 128, NZ * n), F32),
            v((NZ, 2 * NPL, t), BF), v((NZ, NPL, t), F32),
            v((NCH, NPL, CH, d), BF), v((NCH, NPL, CH, d), BF),
            v((NZ, t, d), BF), v((NZ, t, d), BF), v((NZ, 2 * NPL, t), BF),
            v((NCH, NPL, CH, d), BF), v((NCH, NPL, CH, d), BF),
            v((NPL * CH, 512), BF), v((NPL * CH, 512), BF),
            v((slots, f), BF), v((slots, f), BF), v((slots, f), BF),
            v((NCH, NPL, CH, d), BF), v((NCH, NPL, CH, d), BF),
            v((NPL, 1, 128), F32), v((NPL, 1, 128), F32),
            v((NZ, t, d), F32),
            v((3 * n, d), F32), v((3 * n, d), BF),
            v((8, 3 * n, 128), BF), v((4, 3 * n, 128), BF), v((NZ, 3 * n, 128), BF),
            v((NZ, t, d), BF), v((NZ, t, d), BF),
            v((NZ, NPL, t), F32),
            dma, dma, dma, dma, dma, dma,
            dma((2 * NZ,)), dma((2 * NZ,)), dma((NZ,)), dma((NZ,)),
            dma((2, NCH, NPL)), dma((2, NCH, NPL)), dma((NCH + 1, NPL)), dma((NCH + 1, NPL)),
            dma((NPL,)), dma((NPL,)), dma((NZ, 2)), dma((NZ, 2)), dma((NZ,)), dma((NZ,)),
            dma((8,)), dma((8,)), dma((4,)), dma((4,)), dma((NZ,)), dma((NZ,)),
        ],
        compiler_params=pltpu.CompilerParams(
            collective_id=0, has_side_effects=True, vmem_limit_bytes=61 << 20
        ),
        name="layer",
    )(xs, ys, ids, gates, weights, shared)


def finish_kernel(*refs):
    n = 4
    ins, outs, bufs = refs[:n], refs[n : 2 * n], refs[2 * n : 3 * n]
    got, put = refs[3 * n :]
    parts = []
    for i in (2, 3, 0, 1):
        if i >= 2:
            rows = bufs[i].shape[1] // (2 if i == 2 else 1)
            for k in range(bufs[i].shape[0]):
                for r in range(0, bufs[i].shape[1], rows):
                    parts.append((i, (k, slice(r, r + rows))))
        else:
            parts.append((i, (slice(None),)))
    loads = []
    for s, (i, at) in enumerate(parts):
        loads.append(pltpu.make_async_copy(ins[i].at[at], bufs[i].at[at], got.at[s]))
        loads[-1].start()
    stores = []
    for s, (i, at) in enumerate(parts):
        loads[s].wait()
        stores.append(pltpu.make_async_copy(bufs[i].at[at], outs[i].at[at], put.at[s]))
        stores[-1].start()
    for cp in stores:
        cp.wait()


def finish(*arrays):
    hbm = pl.BlockSpec(memory_space=pl.ANY)
    return pl.pallas_call(
        finish_kernel,
        out_shape=tuple(jax.ShapeDtypeStruct(a.shape, a.dtype) for a in arrays),
        in_specs=[hbm] * 4,
        out_specs=(hbm,) * 4,
        scratch_shapes=[pltpu.VMEM(a.shape, a.dtype) for a in arrays]
        + [pltpu.SemaphoreType.DMA((16,)), pltpu.SemaphoreType.DMA((16,))],
        name="finish",
    )(*arrays)


def shards(tokens, cotangent, expert_ids, gate_weights, expert_weights, shared_weights):
    grad_tokens, grad_gates, grad_experts, grad_shared = layer(
        tokens, cotangent, expert_ids.T, gate_weights.T, expert_weights, shared_weights
    )
    grad_tokens, grad_gates, grad_experts, grad_shared = finish(
        grad_tokens, grad_gates, grad_experts, grad_shared
    )
    return (grad_tokens, grad_gates.T, grad_experts[None], grad_shared)


def solution(mesh):
    rows = P(("dp", "expert"), None)
    return jax.shard_map(
        shards,
        mesh=mesh,
        in_specs=(rows, rows, rows, rows, P(("dp", "expert"), None, None, None), P()),
        out_specs=(rows, rows, P(("dp", "expert"), None, None, None), P(None, "dp", None)),
        check_vma=False,
    )
```

time: 197 us -> 159 us (0.81)
  Pallas kernels: 181 us -> 158 us
  local copies, waits for them, and re-layouts: 8.68 us -> 0 us
  other arithmetic: 4.92 us -> 0 us
    pallas_call x1, Pallas kernels: 181 us -> 154 us  [layer(): pl.pallas_call(layer_kernel, out_shape=(jax.ShapeDtypeStruct((t, d), BF),...]
    unnamed x9 -> x0, local copies, waits for them, and re-layouts: 6.39 us -> none
    pallas_call x0 -> x1, Pallas kernels: none -> 3.62 us  [finish(): pl.pallas_call(finish_kernel, out_shape=tuple((jax.ShapeDtypeStruct(a.sha...]
    dynamic_slice x1 -> x0, local copies, waits for them, and re-layouts: 2.29 us -> none  [shards(): sw = lax.dynamic_slice_in_dim(shared_weights, z * f, f, 2)]
    reduce_sum x2 -> x0, other arithmetic: 2 us -> none  [the longest x1 1.11 us: shards(): picked = jnp.sum(jnp.where(match, dgr[None], 0.0), axis=1)]
where the time goes in v3:
time: 159 us; the launch traced here: 158 us
  Pallas kernels  158 us (99%)
    pallas_call x1, Pallas kernels, layer(): pl.pallas_call(layer_kernel, out_shape=(jax.ShapeDtypeStruct((t, d), BF),...  154 us
    pallas_call x1, Pallas kernels, finish(): pl.pallas_call(finish_kernel, out_shape=tuple((jax.ShapeDtypeStruct(a.sha...  3.62 us

profile of v3, /device:TPU:2, one launch (start us, length us, event | category | flops | bytes accessed | tf_op | source)
XLA Modules:
  0.0 158.4 jit_solution(11961249173053348862)
XLA Ops:
  0.6 154.0 %layer.1 = (bf16[128,1024]{1,0:T(8,128)(2,1)}, bf16[10,128]{1,0:T(8,128)(2,1)}, bf16[3,1024,512]{2,1,0:T(8,128)(2,1)}, f32[3,128,512]{2,1,0:T(8,128)}) custom-call(bf16[128,1024]{1,0:T(8,128)(2,1)} %x_hbm.1, bf16[128,1024]{1,0:T(8,128)(2,1)} %y_hbm.1, s32[10,128]{1,0:T(8,128)} %bitcast.4, bf16[10,128]{1,0:T(8,128)(2,1)} %bitcast.5, ...), custom_call_target="tpu_custom_call" | custom-call | tf_op jit(solution)/shard_map/layer/pallas_call | solution.py:451
  154.6 3.6 %finish.1 = (bf16[128,1024]{1,0:T(8,128)(2,1)}, bf16[10,128]{1,0:T(8,128)(2,1)}, bf16[3,1024,512]{2,1,0:T(8,128)(2,1)}, f32[3,128,512]{2,1,0:T(8,128)}) custom-call(bf16[128,1024]{1,0:T(8,128)(2,1)} %get-tuple-element.12.refs_0_, bf16[10,128]{1,0:T(8,128)(2,1)} %get-tuple-element.13.refs_1_, bf16[3,1024,512]{2,1,0:T(8,128)(2,1)} %get-tuple-element.14.refs_2_, ...), custom_call_target="tpu_custom_call" | custom-call | tf_op jit(solution)/shard_map/finish/pallas_call | solution.py:518

commit v4 on v3

--- a/solution.py
+++ b/solution.py
@@ -132,6 +132,17 @@
     greeted()
 
     cps = {}
+    lo = slice(0, d // 2)
+    hi = slice(d // 2, d)
+
+    def go_half(j_to, h):
+        part = (lo, hi)[h]
+        q = POS[j_to]
+        i = 2 * q if h == 0 else (0, 1)[j_to == 7]
+        step = 1 if j_to == 1 else -1
+        cps[(j_to, 0, h)] = start(
+            remote(xg.at[0, :, part], xg.at[q, :, part], zs.at[i], zr.at[i], z_peer(step))
+        )
 
     def go(j_from, j_to, k):
         src = (xg, yg)[k].at[POS[j_from]]
@@ -149,9 +160,11 @@
         metas.append(
             start(remote(rg_ref.at[j], rgo.at[POS[j]], ms.at[j], mr.at[j], z_peer(j)))
         )
-    for k in range(2):
-        go(0, 1, k)
-        go(0, 7, k)
+    for h in range(2):
+        go_half(1, h)
+        go_half(7, h)
+    go(0, 1, 1)
+    go(0, 7, 1)
     rgo[0] = rg_ref[0]
 
     for m in metas:
@@ -159,10 +172,8 @@
 
     rows_in = {chunk: [] for chunk in range(NCH)}
 
-    def pack(chunk, k):
+    def choose(chunk, k):
         q0, q1 = BLOCKS[chunk]
-        width = (q1 - q0) * 128
-        sel, blk, snd, rcv = ((px, xg, sx, rx), (pg, yg, sy, ry))[k]
         for q in range(q0, q1):
             hit = pick(rgo[q, 0:NPL, :].astype(F32), chunk, q)
             if k:
@@ -171,23 +182,30 @@
             else:
                 value = 1.0
             lanes = slice((q - q0) * 128, (q - q0 + 1) * 128)
-            sel[:, lanes] = jnp.where(hit, value, 0.0).astype(BF).reshape(NPL * CH, 128)
+            (px, pg)[k][:, lanes] = jnp.where(hit, value, 0.0).astype(BF).reshape(NPL * CH, 128)
+
+    def pack(chunk, k, part, slot):
+        q0, q1 = BLOCKS[chunk]
+        width = (q1 - q0) * 128
+        cols = part.stop - part.start
+        sel, blk, snd, rcv = ((px, xg, sx, rx), (pg, yg, sy, ry))[k]
 
         def group(g, carry):
             rows = pl.ds(pl.multiple_of(g * 256, 256), 256)
-            got = dot(sel[rows, 0:width], blk[q0:q1].reshape(width, d), 1, 0)
+            got = dot(sel[rows, 0:width], blk[q0:q1, :, part].reshape(width, cols), 1, 0)
             os = pl.ds(pl.multiple_of(g * 16, 16), 16)
-            snd[chunk, os] = got.astype(BF).reshape(16, CH, d)
+            snd[chunk, os, :, part] = got.astype(BF).reshape(16, CH, cols)
             return carry
 
         lax.fori_loop(0, NPL // 16, group, 0)
-        rcv[chunk, 0] = snd[chunk, 0]
+        rcv[chunk, 0, :, part] = snd[chunk, 0, :, part]
         for o in ORDER:
-            sem = (k, chunk, o)
+            sem = (slot, chunk, o)
             rows_in[chunk].append(
                 start(
                     remote(
-                        snd.at[chunk, o], rcv.at[chunk, o], cs.at[sem], cr.at[sem], plane_peer(o)
+                        snd.at[chunk, o, :, part], rcv.at[chunk, o, :, part],
+                        cs.at[sem], cr.at[sem], plane_peer(o),
                     )
                 )
             )
@@ -196,23 +214,36 @@
         arrived((j_from, k))
         go(j_from, j_to, k)
 
-    for k in range(2):
-        forward(1, 2, k)
-        forward(7, 6, k)
-        pack(0, k)
+    full = slice(0, d)
+    choose(0, 0)
+    arrived((1, 0, 0), (7, 0, 0))
+    pack(0, 0, lo, 0)
+    arrived((1, 0, 1))
+    go(1, 2, 0)
+    arrived((7, 0, 1))
+    go(7, 6, 0)
+    pack(0, 0, hi, 2)
+    choose(0, 1)
+    forward(1, 2, 1)
+    forward(7, 6, 1)
+    pack(0, 1, full, 1)
     for k in range(2):
         forward(2, 3, k)
         forward(6, 5, k)
     forward(3, 4, 0)
     arrived((5, 0))
-    pack(1, 0)
+    choose(1, 0)
+    pack(1, 0, full, 0)
     forward(5, 4, 1)
     arrived((3, 1))
-    pack(1, 1)
+    choose(1, 1)
+    pack(1, 1, full, 1)
     arrived((4, 0))
-    pack(2, 0)
+    choose(2, 0)
+    pack(2, 0, full, 0)
     arrived((4, 1))
-    pack(2, 1)
+    choose(2, 1)
+    pack(2, 1, full, 1)
 
     loads.wait()
     n = swb.shape[2] // 2
@@ -273,9 +304,6 @@
         lax.fori_loop(0, 2, group, 0)
 
     rows_back = {}
-
-    lo = slice(0, d // 2)
-    hi = slice(d // 2, d)
 
     def give_back(chunk, sem, part):
         got = []
@@ -346,9 +374,10 @@
     dgot = []
 
     ring = {}
+    parts = [slice(h * d // 4, (h + 1) * d // 4) for h in range(4)]
 
     def hop(j, to, h):
-        part = (lo, hi)[h]
+        part = parts[h]
         to = 4 if j == 7 else to
         ring[(to, h)] = start(
             remote(
@@ -358,28 +387,28 @@
         )
 
     def pass_on(j, h):
-        part = (lo, hi)[h]
+        part = parts[h]
         q = POS[j]
         value = acc[q, :, part]
-        if j != 4 and (j, h) not in ((3, 1), (5, 0)):
+        if j != 4 and (j, h) not in ((3, 2), (3, 3), (5, 0), (5, 1)):
             ring[(j, h)].wait_recv()
             value = value + zin[j, :, part].astype(F32)
         zout[j, :, part] = value.astype(BF)
         if j == 4:
-            hop(j, (3, 5)[h], h)
+            hop(j, (3, 5)[h // 2], h)
         elif j < 4:
             hop(j, j - 1, h)
         else:
             hop(j, (j + 1) % NZ, h)
 
-    def gate_terms(chunk):
+    def gate_terms(chunk, keep):
         spread = jnp.broadcast_to(gsr[...], (NPL, CH, 128))
         value = jnp.sum(jnp.where(lane == row + chunk * CH, spread, 0.0), axis=2, keepdims=True)
         for q in reversed(range(*BLOCKS[chunk])):
             hit = pick(rgo[q, 0:NPL, :].astype(F32), chunk, q)
             i = q - BLOCKS[chunk][0]
             sel = jnp.where(hit, 1.0, 0.0).astype(BF).reshape(NPL * CH, 128)
-            px[:, i * 128 : (i + 1) * 128] = sel
+            keep[:, i * 128 : (i + 1) * 128] = sel
             dterm = jnp.sum(jnp.where(hit, value, 0.0), axis=1)
             dsend[q] = dsend[q] + dterm if q in seen else dterm
             seen.add(q)
@@ -388,27 +417,35 @@
                 j = SEQ[q]
                 dgot.append(start(remote(dsend.at[q], dgo.at[j], ds.at[q], dr.at[q], z_peer(-j))))
 
-    def combine(chunk, sem, part, after):
+    def combine(chunk, sem, keep, part, after):
         for cp in rows_back[sem]:
             cp.wait_recv()
         data = ret[chunk, :, :, part].reshape(NPL * CH, part.stop - part.start)
         for q in reversed(range(*BLOCKS[chunk])):
             i = q - BLOCKS[chunk][0]
-            sel = px[:, i * 128 : (i + 1) * 128]
+            sel = keep[:, i * 128 : (i + 1) * 128]
             acc[q, :, part] = acc[q, :, part] + dot(sel, data, 0, 0)
             for step in after.get(SEQ[q], ()):
                 pass_on(*step)
 
-    full = slice(0, d)
-    gate_terms(1)
-    combine(1, 1, full, {})
-    gate_terms(2)
-    combine(2, 2, full, {4: ((4, 0), (4, 1)), 5: ((5, 0),), 3: ((3, 1),)})
-    for step in ((3, 0), (5, 1), (2, 1), (6, 0), (2, 0), (6, 1)):
+    gate_terms(1, px)
+    gate_terms(2, pg)
+    combine(1, 1, px, full, {})
+    gate_terms(0, px)
+    combine(
+        2, 2, pg, full,
+        {
+            4: ((4, 0), (4, 2), (4, 1), (4, 3)),
+            5: ((5, 0), (5, 1)),
+            3: ((3, 2), (3, 3)),
+        },
+    )
+    for step in ((3, 0), (5, 2), (3, 1), (5, 3), (2, 2), (6, 0), (2, 3), (6, 1)):
         pass_on(*step)
-    gate_terms(0)
-    combine(0, 0, lo, {7: ((7, 0),), 1: ((1, 0),)})
-    combine(0, NCH, hi, {7: ((7, 1),), 1: ((1, 1),)})
+    for step in ((2, 0), (6, 2), (2, 1), (6, 3)):
+        pass_on(*step)
+    combine(0, 0, px, lo, {7: ((7, 0), (7, 1)), 1: ((1, 0), (1, 1))})
+    combine(0, NCH, px, hi, {7: ((7, 2), (7, 3)), 1: ((1, 2), (1, 3))})
     dgo[0] = dsend[0]
     for cp in part3:
         cp.wait_recv()
@@ -428,7 +465,7 @@
         gate = gw_ref[k : k + 1, :].astype(F32)
         rows.append(jnp.sum(total, axis=0, keepdims=True) / gate)
     ggo[...] = jnp.concatenate(rows, axis=0).astype(BF)
-    for h, part in enumerate((lo, hi)):
+    for h, part in enumerate(parts):
         ring[(4, h)].wait_recv()
         ring[(0, h)].wait_recv()
         total = acc[0, :, part] + zin[0, :, part].astype(F32) + zin[4, :, part].astype(F32)
@@ -476,8 +513,8 @@
             v((NZ, NPL, t), F32),
             dma, dma, dma, dma, dma, dma,
             dma((2 * NZ,)), dma((2 * NZ,)), dma((NZ,)), dma((NZ,)),
-            dma((2, NCH, NPL)), dma((2, NCH, NPL)), dma((NCH + 1, NPL)), dma((NCH + 1, NPL)),
-            dma((NPL,)), dma((NPL,)), dma((NZ, 2)), dma((NZ, 2)), dma((NZ,)), dma((NZ,)),
+            dma((3, NCH, NPL)), dma((3, NCH, NPL)), dma((NCH + 1, NPL)), dma((NCH + 1, NPL)),
+            dma((NPL,)), dma((NPL,)), dma((NZ, 4)), dma((NZ, 4)), dma((NZ,)), dma((NZ,)),
             dma((8,)), dma((8,)), dma((4,)), dma((4,)), dma((NZ,)), dma((NZ,)),
         ],
         compiler_params=pltpu.CompilerParams(

time: 159 us -> 161 us (1.013)
  Pallas kernels: 158 us -> 160 us
    pallas_call x1, Pallas kernels: 154 us -> 156 us  [layer(): pl.pallas_call(layer_kernel, out_shape=(jax.ShapeDtypeStruct((t, d), BF),...]
where the time goes in v4:
time: 161 us
  Pallas kernels  160 us (99%)
    pallas_call x1, Pallas kernels, layer(): pl.pallas_call(layer_kernel, out_shape=(jax.ShapeDtypeStruct((t, d), BF),...  156 us
    pallas_call x1, Pallas kernels, finish(): pl.pallas_call(finish_kernel, out_shape=tuple((jax.ShapeDtypeStruct(a.sha...  3.62 us

profile of v4, /device:TPU:2, one launch (start us, length us, event | category | flops | bytes accessed | tf_op | source)
XLA Modules:
  0.0 160.5 jit_solution(14427512714909993959)
XLA Ops:
  0.6 156.1 %layer.1 = (bf16[128,1024]{1,0:T(8,128)(2,1)}, bf16[10,128]{1,0:T(8,128)(2,1)}, bf16[3,1024,512]{2,1,0:T(8,128)(2,1)}, f32[3,128,512]{2,1,0:T(8,128)}) custom-call(bf16[128,1024]{1,0:T(8,128)(2,1)} %x_hbm.1, bf16[128,1024]{1,0:T(8,128)(2,1)} %y_hbm.1, s32[10,128]{1,0:T(8,128)} %bitcast.4, bf16[10,128]{1,0:T(8,128)(2,1)} %bitcast.5, ...), custom_call_target="tpu_custom_call" | custom-call | tf_op jit(solution)/shard_map/layer/pallas_call | solution.py:488
  156.8 3.6 %finish.1 = (bf16[128,1024]{1,0:T(8,128)(2,1)}, bf16[10,128]{1,0:T(8,128)(2,1)}, bf16[3,1024,512]{2,1,0:T(8,128)(2,1)}, f32[3,128,512]{2,1,0:T(8,128)}) custom-call(bf16[128,1024]{1,0:T(8,128)(2,1)} %get-tuple-element.12.refs_0_, bf16[10,128]{1,0:T(8,128)(2,1)} %get-tuple-element.13.refs_1_, bf16[3,1024,512]{2,1,0:T(8,128)(2,1)} %get-tuple-element.14.refs_2_, ...), custom_call_target="tpu_custom_call" | custom-call | tf_op jit(solution)/shard_map/finish/pallas_call | solution.py:555

commit v5 on v3

--- a/solution.py
+++ b/solution.py
@@ -323,9 +323,7 @@
         ge[2, cols, :] = dot(by, hid[...], 0, 0).astype(BF)
         return carry
 
-    lax.fori_loop(0, d // 256, wgrad, 0)
-    save = pltpu.make_async_copy(ge, ge_hbm, gsem)
-    save.start()
+    lax.fori_loop(0, d // 512, wgrad, 0)
 
     for cp in part2:
         cp.wait_recv()
@@ -404,7 +402,13 @@
     combine(1, 1, full, {})
     gate_terms(2)
     combine(2, 2, full, {4: ((4, 0), (4, 1)), 5: ((5, 0),), 3: ((3, 1),)})
-    for step in ((3, 0), (5, 1), (2, 1), (6, 0), (2, 0), (6, 1)):
+    lax.fori_loop(d // 512, d // 512 + 1, wgrad, 0)
+    for step in ((3, 0), (5, 1), (2, 1), (6, 0)):
+        pass_on(*step)
+    lax.fori_loop(d // 512 + 1, d // 256, wgrad, 0)
+    save = pltpu.make_async_copy(ge, ge_hbm, gsem)
+    save.start()
+    for step in ((2, 0), (6, 1)):
         pass_on(*step)
     gate_terms(0)
     combine(0, 0, lo, {7: ((7, 0),), 1: ((1, 0),)})

time: 159 us -> 159 us (level)
  no operation moved by 1% of the time
where the time goes in v5:
time: 159 us
  Pallas kernels  158 us (99%)
    pallas_call x1, Pallas kernels, layer(): pl.pallas_call(layer_kernel, out_shape=(jax.ShapeDtypeStruct((t, d), BF),...  155 us
    pallas_call x1, Pallas kernels, finish(): pl.pallas_call(finish_kernel, out_shape=tuple((jax.ShapeDtypeStruct(a.sha...  3.62 us

profile of v5, /device:TPU:2, one launch (start us, length us, event | category | flops | bytes accessed | tf_op | source)
XLA Modules:
  0.0 159.0 jit_solution(16011042561668062738)
XLA Ops:
  0.6 154.6 %layer.1 = (bf16[128,1024]{1,0:T(8,128)(2,1)}, bf16[10,128]{1,0:T(8,128)(2,1)}, bf16[3,1024,512]{2,1,0:T(8,128)(2,1)}, f32[3,128,512]{2,1,0:T(8,128)}) custom-call(bf16[128,1024]{1,0:T(8,128)(2,1)} %x_hbm.1, bf16[128,1024]{1,0:T(8,128)(2,1)} %y_hbm.1, s32[10,128]{1,0:T(8,128)} %bitcast.4, bf16[10,128]{1,0:T(8,128)(2,1)} %bitcast.5, ...), custom_call_target="tpu_custom_call" | custom-call | tf_op jit(solution)/shard_map/layer/pallas_call | solution.py:455
  155.2 3.6 %finish.1 = (bf16[128,1024]{1,0:T(8,128)(2,1)}, bf16[10,128]{1,0:T(8,128)(2,1)}, bf16[3,1024,512]{2,1,0:T(8,128)(2,1)}, f32[3,128,512]{2,1,0:T(8,128)}) custom-call(bf16[128,1024]{1,0:T(8,128)(2,1)} %get-tuple-element.12.refs_0_, bf16[10,128]{1,0:T(8,128)(2,1)} %get-tuple-element.13.refs_1_, bf16[3,1024,512]{2,1,0:T(8,128)(2,1)} %get-tuple-element.14.refs_2_, ...), custom_call_target="tpu_custom_call" | custom-call | tf_op jit(solution)/shard_map/finish/pallas_call | solution.py:522
